TPU v7x, 16 devices: a whole 2x2x2 slice. The times are simulated.
16 devices in a mesh: dp: 16 (over z, y, x, core).
Axes of the slice: x: 2, y: 2, z: 2, core: 2. Of those that a mesh axis runs over, the one named last changes fastest.
Arguments:
- img_emb: bfloat16 [24576, 1536], P('dp')
- txt_emb: bfloat16 [24576, 1536], P('dp')
- log_temp: float32 [1], replicated
- logit_bias: float32 [1], replicated
Outputs:
- output 1: float32 [1], replicated
- output 2: float32 [24576, 1536], P('dp')
- output 3: float32 [24576, 1536], P('dp')
- output 4: float32 [1], replicated
- output 5: float32 [1], replicated
All inputs are finite; a program needn't handle non-finite values.
Results may differ from a plain program's by a relative error of at most 0.001.
Values are sent between devices in bfloat16 or wider.
A program may use at most 1 GiB of HBM per device.

v0:
```python
import jax
import jax.numpy as jnp
from jax import lax
from jax.sharding import PartitionSpec as P


def block_terms(img_local, txt_block, labels, temp_scale, bias_val):
    dot_vals = jnp.einsum('id,jd->ij', img_local, txt_block, preferred_element_type=jnp.float32)
    margin = labels * (temp_scale * dot_vals + bias_val)
    loss_part = jnp.sum(jax.nn.softplus(-margin))
    grad_coef = -labels * jax.nn.sigmoid(-margin)
    coef_bf16 = grad_coef.astype(jnp.bfloat16)
    img_part = jnp.einsum('ij,jd->id', coef_bf16, txt_block, preferred_element_type=jnp.float32)
    txt_part = jnp.einsum('ij,id->jd', coef_bf16, img_local, preferred_element_type=jnp.float32)
    return loss_part, jnp.sum(grad_coef), jnp.sum(grad_coef * dot_vals), img_part, txt_part


def solution(mesh):
    axis_name = mesh.axis_names[0]
    n_dev = mesh.shape[axis_name]
    shift_pairs = [(source, (source - 1) % n_dev) for source in range(n_dev)]

    def per_device(img_local, txt_local, log_temp, logit_bias):
        local_rows = img_local.shape[0]
        n_total = local_rows * n_dev
        temp_scale = jnp.exp(log_temp[0])
        bias_val = logit_bias[0]
        row_ids = jnp.arange(local_rows)
        diag_labels = jnp.where(row_ids[:, None] == row_ids[None, :], 1.0, -1.0)
        first_terms = block_terms(img_local, txt_local, diag_labels, temp_scale, bias_val)

        def step_fn(step_idx, loop_state):
            txt_block, txt_acc, loss_acc, bias_acc, temp_acc, img_acc = loop_state
            txt_block = lax.ppermute(txt_block, axis_name, shift_pairs)
            txt_acc = lax.ppermute(txt_acc, axis_name, shift_pairs)
            loss_part, bias_part, temp_part, img_part, txt_part = block_terms(img_local, txt_block, -1.0, temp_scale, bias_val)
            return (txt_block, txt_acc + txt_part, loss_acc + loss_part, bias_acc + bias_part, temp_acc + temp_part, img_acc + img_part)

        init_state = (txt_local, first_terms[4], first_terms[0], first_terms[1], first_terms[2], first_terms[3])
        final_state = lax.fori_loop(1, n_dev, step_fn, init_state)
        txt_acc = lax.ppermute(final_state[1], axis_name, shift_pairs)
        global_sums = lax.psum(jnp.stack([final_state[2], final_state[3], final_state[4]]), axis_name)
        factor = temp_scale / n_total
        return (global_sums[0:1] / n_total, final_state[5] * factor, txt_acc * factor, global_sums[2:3] * factor, global_sums[1:2] / n_total)

    return jax.shard_map(per_device, mesh=mesh, in_specs=(P(axis_name, None), P(axis_name, None), P(None), P(None)), out_specs=(P(None), P(axis_name, None), P(axis_name, None), P(None), P(None)), check_vma=False)
```

profile of v0, /device:TPU:0, one launch (start us, length us, event | category | flops | bytes accessed | tf_op | source)
XLA Modules:
  0.0 2766.4 jit_solution(9453519465652345993)
XLA Ops:
  47.4 2563.3 %while.20 = (s32[]{:T(128)}, bf16[1536,1536]{1,0:T(8,128)(2,1)}, f32[1536,1536]{1,0:T(8,128)}, f32[]{:T(128)}, f32[]{:T(128)}, /*index=5*/f32[]{:T(128)}, f32[15...) while((s32[]{:T(128)}, bf16[1536,1536]{1,0:T(8,128)(2,1)}, ...), condition=%wide.region_7.8_spmd, body=%wide.region_3.7_spmd.sunk | while | flops 21814050816 | bytes 193462672 | solution.py:40
  150.6 54.1 %collective-permute-done.1 = f32[1536,1536]{1,0:T(8,128)} collective-permute-done((f32[1536,1536]{1,0:T(8,128)}, f32[1536,1536]{1,0:T(8,128)}, u32[]{:S(2)}, u32[]{:S(2)}) %collective-permute-start.1) | collective-permute-done | bytes 9437216 | tf_op jit(solution)/shard_map/while/body/eval_jaxpr/ppermute | solution.py:35
  222.9 51.6 %collective-permute-done = bf16[1536,1536]{1,0:T(8,128)(2,1)} collective-permute-done((bf16[1536,1536]{1,0:T(8,128)(2,1)}, bf16[1536,1536]{1,0:T(8,128)(2,1)}, u32[]{:S(2)}, u32[]{:S(2)}) %collective-permute-start) | collective-permute-done | bytes 4718624 | tf_op jit(solution)/shard_map/while/body/eval_jaxpr/ppermute | solution.py:34
  321.4 54.1 %collective-permute-done.1 = f32[1536,1536]{1,0:T(8,128)} collective-permute-done((f32[1536,1536]{1,0:T(8,128)}, f32[1536,1536]{1,0:T(8,128)}, u32[]{:S(2)}, u32[]{:S(2)}) %collective-permute-start.1) | collective-permute-done | bytes 9437216 | tf_op jit(solution)/shard_map/while/body/eval_jaxpr/ppermute | solution.py:35
  393.7 51.6 %collective-permute-done = bf16[1536,1536]{1,0:T(8,128)(2,1)} collective-permute-done((bf16[1536,1536]{1,0:T(8,128)(2,1)}, bf16[1536,1536]{1,0:T(8,128)(2,1)}, u32[]{:S(2)}, u32[]{:S(2)}) %collective-permute-start) | collective-permute-done | bytes 4718624 | tf_op jit(solution)/shard_map/while/body/eval_jaxpr/ppermute | solution.py:34
  492.3 54.1 %collective-permute-done.1 = f32[1536,1536]{1,0:T(8,128)} collective-permute-done((f32[1536,1536]{1,0:T(8,128)}, f32[1536,1536]{1,0:T(8,128)}, u32[]{:S(2)}, u32[]{:S(2)}) %collective-permute-start.1) | collective-permute-done | bytes 9437216 | tf_op jit(solution)/shard_map/while/body/eval_jaxpr/ppermute | solution.py:35
  564.5 51.6 %collective-permute-done = bf16[1536,1536]{1,0:T(8,128)(2,1)} collective-permute-done((bf16[1536,1536]{1,0:T(8,128)(2,1)}, bf16[1536,1536]{1,0:T(8,128)(2,1)}, u32[]{:S(2)}, u32[]{:S(2)}) %collective-permute-start) | collective-permute-done | bytes 4718624 | tf_op jit(solution)/shard_map/while/body/eval_jaxpr/ppermute | solution.py:34
  663.1 54.1 %collective-permute-done.1 = f32[1536,1536]{1,0:T(8,128)} collective-permute-done((f32[1536,1536]{1,0:T(8,128)}, f32[1536,1536]{1,0:T(8,128)}, u32[]{:S(2)}, u32[]{:S(2)}) %collective-permute-start.1) | collective-permute-done | bytes 9437216 | tf_op jit(solution)/shard_map/while/body/eval_jaxpr/ppermute | solution.py:35
  735.3 51.6 %collective-permute-done = bf16[1536,1536]{1,0:T(8,128)(2,1)} collective-permute-done((bf16[1536,1536]{1,0:T(8,128)(2,1)}, bf16[1536,1536]{1,0:T(8,128)(2,1)}, u32[]{:S(2)}, u32[]{:S(2)}) %collective-permute-start) | collective-permute-done | bytes 4718624 | tf_op jit(solution)/shard_map/while/body/eval_jaxpr/ppermute | solution.py:34
  833.9 54.1 %collective-permute-done.1 = f32[1536,1536]{1,0:T(8,128)} collective-permute-done((f32[1536,1536]{1,0:T(8,128)}, f32[1536,1536]{1,0:T(8,128)}, u32[]{:S(2)}, u32[]{:S(2)}) %collective-permute-start.1) | collective-permute-done | bytes 9437216 | tf_op jit(solution)/shard_map/while/body/eval_jaxpr/ppermute | solution.py:35
  1004.7 54.1 %collective-permute-done.1 = f32[1536,1536]{1,0:T(8,128)} collective-permute-done((f32[1536,1536]{1,0:T(8,128)}, f32[1536,1536]{1,0:T(8,128)}, u32[]{:S(2)}, u32[]{:S(2)}) %collective-permute-start.1) | collective-permute-done | bytes 9437216 | tf_op jit(solution)/shard_map/while/body/eval_jaxpr/ppermute | solution.py:35
  1077.0 51.6 %collective-permute-done = bf16[1536,1536]{1,0:T(8,128)(2,1)} collective-permute-done((bf16[1536,1536]{1,0:T(8,128)(2,1)}, bf16[1536,1536]{1,0:T(8,128)(2,1)}, u32[]{:S(2)}, u32[]{:S(2)}) %collective-permute-start) | collective-permute-done | bytes 4718624 | tf_op jit(solution)/shard_map/while/body/eval_jaxpr/ppermute | solution.py:34
  1175.6 54.1 %collective-permute-done.1 = f32[1536,1536]{1,0:T(8,128)} collective-permute-done((f32[1536,1536]{1,0:T(8,128)}, f32[1536,1536]{1,0:T(8,128)}, u32[]{:S(2)}, u32[]{:S(2)}) %collective-permute-start.1) | collective-permute-done | bytes 9437216 | tf_op jit(solution)/shard_map/while/body/eval_jaxpr/ppermute | solution.py:35
  1247.8 51.6 %collective-permute-done = bf16[1536,1536]{1,0:T(8,128)(2,1)} collective-permute-done((bf16[1536,1536]{1,0:T(8,128)(2,1)}, bf16[1536,1536]{1,0:T(8,128)(2,1)}, u32[]{:S(2)}, u32[]{:S(2)}) %collective-permute-start) | collective-permute-done | bytes 4718624 | tf_op jit(solution)/shard_map/while/body/eval_jaxpr/ppermute | solution.py:34
  1346.4 54.1 %collective-permute-done.1 = f32[1536,1536]{1,0:T(8,128)} collective-permute-done((f32[1536,1536]{1,0:T(8,128)}, f32[1536,1536]{1,0:T(8,128)}, u32[]{:S(2)}, u32[]{:S(2)}) %collective-permute-start.1) | collective-permute-done | bytes 9437216 | tf_op jit(solution)/shard_map/while/body/eval_jaxpr/ppermute | solution.py:35
  1517.2 54.1 %collective-permute-done.1 = f32[1536,1536]{1,0:T(8,128)} collective-permute-done((f32[1536,1536]{1,0:T(8,128)}, f32[1536,1536]{1,0:T(8,128)}, u32[]{:S(2)}, u32[]{:S(2)}) %collective-permute-start.1) | collective-permute-done | bytes 9437216 | tf_op jit(solution)/shard_map/while/body/eval_jaxpr/ppermute | solution.py:35
  1688.1 54.1 %collective-permute-done.1 = f32[1536,1536]{1,0:T(8,128)} collective-permute-done((f32[1536,1536]{1,0:T(8,128)}, f32[1536,1536]{1,0:T(8,128)}, u32[]{:S(2)}, u32[]{:S(2)}) %collective-permute-start.1) | collective-permute-done | bytes 9437216 | tf_op jit(solution)/shard_map/while/body/eval_jaxpr/ppermute | solution.py:35
  1858.9 54.1 %collective-permute-done.1 = f32[1536,1536]{1,0:T(8,128)} collective-permute-done((f32[1536,1536]{1,0:T(8,128)}, f32[1536,1536]{1,0:T(8,128)}, u32[]{:S(2)}, u32[]{:S(2)}) %collective-permute-start.1) | collective-permute-done | bytes 9437216 | tf_op jit(solution)/shard_map/while/body/eval_jaxpr/ppermute | solution.py:35
  2029.7 54.1 %collective-permute-done.1 = f32[1536,1536]{1,0:T(8,128)} collective-permute-done((f32[1536,1536]{1,0:T(8,128)}, f32[1536,1536]{1,0:T(8,128)}, u32[]{:S(2)}, u32[]{:S(2)}) %collective-permute-start.1) | collective-permute-done | bytes 9437216 | tf_op jit(solution)/shard_map/while/body/eval_jaxpr/ppermute | solution.py:35
  2102.0 51.6 %collective-permute-done = bf16[1536,1536]{1,0:T(8,128)(2,1)} collective-permute-done((bf16[1536,1536]{1,0:T(8,128)(2,1)}, bf16[1536,1536]{1,0:T(8,128)(2,1)}, u32[]{:S(2)}, u32[]{:S(2)}) %collective-permute-start) | collective-permute-done | bytes 4718624 | tf_op jit(solution)/shard_map/while/body/eval_jaxpr/ppermute | solution.py:34
  2200.5 54.1 %collective-permute-done.1 = f32[1536,1536]{1,0:T(8,128)} collective-permute-done((f32[1536,1536]{1,0:T(8,128)}, f32[1536,1536]{1,0:T(8,128)}, u32[]{:S(2)}, u32[]{:S(2)}) %collective-permute-start.1) | collective-permute-done | bytes 9437216 | tf_op jit(solution)/shard_map/while/body/eval_jaxpr/ppermute | solution.py:35
  2371.4 54.1 %collective-permute-done.1 = f32[1536,1536]{1,0:T(8,128)} collective-permute-done((f32[1536,1536]{1,0:T(8,128)}, f32[1536,1536]{1,0:T(8,128)}, u32[]{:S(2)}, u32[]{:S(2)}) %collective-permute-start.1) | collective-permute-done | bytes 9437216 | tf_op jit(solution)/shard_map/while/body/eval_jaxpr/ppermute | solution.py:35
  2542.2 54.1 %collective-permute-done.1 = f32[1536,1536]{1,0:T(8,128)} collective-permute-done((f32[1536,1536]{1,0:T(8,128)}, f32[1536,1536]{1,0:T(8,128)}, u32[]{:S(2)}, u32[]{:S(2)}) %collective-permute-start.1) | collective-permute-done | bytes 9437216 | tf_op jit(solution)/shard_map/while/body/eval_jaxpr/ppermute | solution.py:35
  2616.4 127.1 %psum.7 = f32[3]{0:T(128)S(1)} all-reduce(f32[3]{0:T(128)S(1)} %pad_maximum_fusion), channel_id=1, replica_groups=mesh['dp'=16] {'dp'}, use_global_device_ids=true, to_apply=%region_8.9 | all-reduce | flops 3 | bytes 24 | tf_op jit(solution)/shard_map/psum | solution.py:42
  (292 shorter events, 1375.6 us)
Async XLA Ops:
  47.4 56.3 %collective-permute-start = (bf16[1536,1536]{1,0:T(8,128)(2,1)}, bf16[1536,1536]{1,0:T(8,128)(2,1)}, u32[]{:S(2)}, u32[]{:S(2)}) collective-permute-start(bf16[1536,1536]{1,0:T(8,128)(2,1)} %get-tuple-element.178), channel_id=1, source_target_pairs={{0,15},{1,0},{2,1},{3,2},{4,3},{5,4},{6,5},{7,6},{8,7},{9,8},{10,9... | collective-permute-start | bytes 14155784 | tf_op jit(solution)/shard_map/while/body/eval_jaxpr/ppermute | solution.py:34
  52.0 152.7 %collective-permute-start.1 = (f32[1536,1536]{1,0:T(8,128)}, f32[1536,1536]{1,0:T(8,128)}, u32[]{:S(2)}, u32[]{:S(2)}) collective-permute-start(f32[1536,1536]{1,0:T(8,128)} %get-tuple-element.179), channel_id=1, source_target_pairs={{0,15},{1,0},{2,1},{3,2},{4,3},{5,4},{6,5},{7,6},{8,7},{9,8},{10,9... | collective-permute-start | bytes 28311560 | tf_op jit(solution)/shard_map/while/body/eval_jaxpr/ppermute | solution.py:35
  222.8 152.7 %collective-permute-start.1 = (f32[1536,1536]{1,0:T(8,128)}, f32[1536,1536]{1,0:T(8,128)}, u32[]{:S(2)}, u32[]{:S(2)}) collective-permute-start(f32[1536,1536]{1,0:T(8,128)} %get-tuple-element.179), channel_id=1, source_target_pairs={{0,15},{1,0},{2,1},{3,2},{4,3},{5,4},{6,5},{7,6},{8,7},{9,8},{10,9... | collective-permute-start | bytes 28311560 | tf_op jit(solution)/shard_map/while/body/eval_jaxpr/ppermute | solution.py:35
  389.9 55.4 %collective-permute-start = (bf16[1536,1536]{1,0:T(8,128)(2,1)}, bf16[1536,1536]{1,0:T(8,128)(2,1)}, u32[]{:S(2)}, u32[]{:S(2)}) collective-permute-start(bf16[1536,1536]{1,0:T(8,128)(2,1)} %get-tuple-element.178), channel_id=1, source_target_pairs={{0,15},{1,0},{2,1},{3,2},{4,3},{5,4},{6,5},{7,6},{8,7},{9,8},{10,9... | collective-permute-start | bytes 14155784 | tf_op jit(solution)/shard_map/while/body/eval_jaxpr/ppermute | solution.py:34
  393.6 152.7 %collective-permute-start.1 = (f32[1536,1536]{1,0:T(8,128)}, f32[1536,1536]{1,0:T(8,128)}, u32[]{:S(2)}, u32[]{:S(2)}) collective-permute-start(f32[1536,1536]{1,0:T(8,128)} %get-tuple-element.179), channel_id=1, source_target_pairs={{0,15},{1,0},{2,1},{3,2},{4,3},{5,4},{6,5},{7,6},{8,7},{9,8},{10,9... | collective-permute-start | bytes 28311560 | tf_op jit(solution)/shard_map/while/body/eval_jaxpr/ppermute | solution.py:35
  564.5 152.7 %collective-permute-start.1 = (f32[1536,1536]{1,0:T(8,128)}, f32[1536,1536]{1,0:T(8,128)}, u32[]{:S(2)}, u32[]{:S(2)}) collective-permute-start(f32[1536,1536]{1,0:T(8,128)} %get-tuple-element.179), channel_id=1, source_target_pairs={{0,15},{1,0},{2,1},{3,2},{4,3},{5,4},{6,5},{7,6},{8,7},{9,8},{10,9... | collective-permute-start | bytes 28311560 | tf_op jit(solution)/shard_map/while/body/eval_jaxpr/ppermute | solution.py:35
  731.6 55.4 %collective-permute-start = (bf16[1536,1536]{1,0:T(8,128)(2,1)}, bf16[1536,1536]{1,0:T(8,128)(2,1)}, u32[]{:S(2)}, u32[]{:S(2)}) collective-permute-start(bf16[1536,1536]{1,0:T(8,128)(2,1)} %get-tuple-element.178), channel_id=1, source_target_pairs={{0,15},{1,0},{2,1},{3,2},{4,3},{5,4},{6,5},{7,6},{8,7},{9,8},{10,9... | collective-permute-start | bytes 14155784 | tf_op jit(solution)/shard_map/while/body/eval_jaxpr/ppermute | solution.py:34
  735.3 152.7 %collective-permute-start.1 = (f32[1536,1536]{1,0:T(8,128)}, f32[1536,1536]{1,0:T(8,128)}, u32[]{:S(2)}, u32[]{:S(2)}) collective-permute-start(f32[1536,1536]{1,0:T(8,128)} %get-tuple-element.179), channel_id=1, source_target_pairs={{0,15},{1,0},{2,1},{3,2},{4,3},{5,4},{6,5},{7,6},{8,7},{9,8},{10,9... | collective-permute-start | bytes 28311560 | tf_op jit(solution)/shard_map/while/body/eval_jaxpr/ppermute | solution.py:35
  906.1 152.7 %collective-permute-start.1 = (f32[1536,1536]{1,0:T(8,128)}, f32[1536,1536]{1,0:T(8,128)}, u32[]{:S(2)}, u32[]{:S(2)}) collective-permute-start(f32[1536,1536]{1,0:T(8,128)} %get-tuple-element.179), channel_id=1, source_target_pairs={{0,15},{1,0},{2,1},{3,2},{4,3},{5,4},{6,5},{7,6},{8,7},{9,8},{10,9... | collective-permute-start | bytes 28311560 | tf_op jit(solution)/shard_map/while/body/eval_jaxpr/ppermute | solution.py:35
  1073.2 55.4 %collective-permute-start = (bf16[1536,1536]{1,0:T(8,128)(2,1)}, bf16[1536,1536]{1,0:T(8,128)(2,1)}, u32[]{:S(2)}, u32[]{:S(2)}) collective-permute-start(bf16[1536,1536]{1,0:T(8,128)(2,1)} %get-tuple-element.178), channel_id=1, source_target_pairs={{0,15},{1,0},{2,1},{3,2},{4,3},{5,4},{6,5},{7,6},{8,7},{9,8},{10,9... | collective-permute-start | bytes 14155784 | tf_op jit(solution)/shard_map/while/body/eval_jaxpr/ppermute | solution.py:34
  1077.0 152.7 %collective-permute-start.1 = (f32[1536,1536]{1,0:T(8,128)}, f32[1536,1536]{1,0:T(8,128)}, u32[]{:S(2)}, u32[]{:S(2)}) collective-permute-start(f32[1536,1536]{1,0:T(8,128)} %get-tuple-element.179), channel_id=1, source_target_pairs={{0,15},{1,0},{2,1},{3,2},{4,3},{5,4},{6,5},{7,6},{8,7},{9,8},{10,9... | collective-permute-start | bytes 28311560 | tf_op jit(solution)/shard_map/while/body/eval_jaxpr/ppermute | solution.py:35
  1247.8 152.7 %collective-permute-start.1 = (f32[1536,1536]{1,0:T(8,128)}, f32[1536,1536]{1,0:T(8,128)}, u32[]{:S(2)}, u32[]{:S(2)}) collective-permute-start(f32[1536,1536]{1,0:T(8,128)} %get-tuple-element.179), channel_id=1, source_target_pairs={{0,15},{1,0},{2,1},{3,2},{4,3},{5,4},{6,5},{7,6},{8,7},{9,8},{10,9... | collective-permute-start | bytes 28311560 | tf_op jit(solution)/shard_map/while/body/eval_jaxpr/ppermute | solution.py:35
  1414.9 55.4 %collective-permute-start = (bf16[1536,1536]{1,0:T(8,128)(2,1)}, bf16[1536,1536]{1,0:T(8,128)(2,1)}, u32[]{:S(2)}, u32[]{:S(2)}) collective-permute-start(bf16[1536,1536]{1,0:T(8,128)(2,1)} %get-tuple-element.178), channel_id=1, source_target_pairs={{0,15},{1,0},{2,1},{3,2},{4,3},{5,4},{6,5},{7,6},{8,7},{9,8},{10,9... | collective-permute-start | bytes 14155784 | tf_op jit(solution)/shard_map/while/body/eval_jaxpr/ppermute | solution.py:34
  1418.6 152.7 %collective-permute-start.1 = (f32[1536,1536]{1,0:T(8,128)}, f32[1536,1536]{1,0:T(8,128)}, u32[]{:S(2)}, u32[]{:S(2)}) collective-permute-start(f32[1536,1536]{1,0:T(8,128)} %get-tuple-element.179), channel_id=1, source_target_pairs={{0,15},{1,0},{2,1},{3,2},{4,3},{5,4},{6,5},{7,6},{8,7},{9,8},{10,9... | collective-permute-start | bytes 28311560 | tf_op jit(solution)/shard_map/while/body/eval_jaxpr/ppermute | solution.py:35
  1589.4 152.7 %collective-permute-start.1 = (f32[1536,1536]{1,0:T(8,128)}, f32[1536,1536]{1,0:T(8,128)}, u32[]{:S(2)}, u32[]{:S(2)}) collective-permute-start(f32[1536,1536]{1,0:T(8,128)} %get-tuple-element.179), channel_id=1, source_target_pairs={{0,15},{1,0},{2,1},{3,2},{4,3},{5,4},{6,5},{7,6},{8,7},{9,8},{10,9... | collective-permute-start | bytes 28311560 | tf_op jit(solution)/shard_map/while/body/eval_jaxpr/ppermute | solution.py:35
  1756.5 55.4 %collective-permute-start = (bf16[1536,1536]{1,0:T(8,128)(2,1)}, bf16[1536,1536]{1,0:T(8,128)(2,1)}, u32[]{:S(2)}, u32[]{:S(2)}) collective-permute-start(bf16[1536,1536]{1,0:T(8,128)(2,1)} %get-tuple-element.178), channel_id=1, source_target_pairs={{0,15},{1,0},{2,1},{3,2},{4,3},{5,4},{6,5},{7,6},{8,7},{9,8},{10,9... | collective-permute-start | bytes 14155784 | tf_op jit(solution)/shard_map/while/body/eval_jaxpr/ppermute | solution.py:34
  1760.3 152.7 %collective-permute-start.1 = (f32[1536,1536]{1,0:T(8,128)}, f32[1536,1536]{1,0:T(8,128)}, u32[]{:S(2)}, u32[]{:S(2)}) collective-permute-start(f32[1536,1536]{1,0:T(8,128)} %get-tuple-element.179), channel_id=1, source_target_pairs={{0,15},{1,0},{2,1},{3,2},{4,3},{5,4},{6,5},{7,6},{8,7},{9,8},{10,9... | collective-permute-start | bytes 28311560 | tf_op jit(solution)/shard_map/while/body/eval_jaxpr/ppermute | solution.py:35
  1931.1 152.7 %collective-permute-start.1 = (f32[1536,1536]{1,0:T(8,128)}, f32[1536,1536]{1,0:T(8,128)}, u32[]{:S(2)}, u32[]{:S(2)}) collective-permute-start(f32[1536,1536]{1,0:T(8,128)} %get-tuple-element.179), channel_id=1, source_target_pairs={{0,15},{1,0},{2,1},{3,2},{4,3},{5,4},{6,5},{7,6},{8,7},{9,8},{10,9... | collective-permute-start | bytes 28311560 | tf_op jit(solution)/shard_map/while/body/eval_jaxpr/ppermute | solution.py:35
  2098.2 55.4 %collective-permute-start = (bf16[1536,1536]{1,0:T(8,128)(2,1)}, bf16[1536,1536]{1,0:T(8,128)(2,1)}, u32[]{:S(2)}, u32[]{:S(2)}) collective-permute-start(bf16[1536,1536]{1,0:T(8,128)(2,1)} %get-tuple-element.178), channel_id=1, source_target_pairs={{0,15},{1,0},{2,1},{3,2},{4,3},{5,4},{6,5},{7,6},{8,7},{9,8},{10,9... | collective-permute-start | bytes 14155784 | tf_op jit(solution)/shard_map/while/body/eval_jaxpr/ppermute | solution.py:34
  2101.9 152.7 %collective-permute-start.1 = (f32[1536,1536]{1,0:T(8,128)}, f32[1536,1536]{1,0:T(8,128)}, u32[]{:S(2)}, u32[]{:S(2)}) collective-permute-start(f32[1536,1536]{1,0:T(8,128)} %get-tuple-element.179), channel_id=1, source_target_pairs={{0,15},{1,0},{2,1},{3,2},{4,3},{5,4},{6,5},{7,6},{8,7},{9,8},{10,9... | collective-permute-start | bytes 28311560 | tf_op jit(solution)/shard_map/while/body/eval_jaxpr/ppermute | solution.py:35
  2272.8 152.7 %collective-permute-start.1 = (f32[1536,1536]{1,0:T(8,128)}, f32[1536,1536]{1,0:T(8,128)}, u32[]{:S(2)}, u32[]{:S(2)}) collective-permute-start(f32[1536,1536]{1,0:T(8,128)} %get-tuple-element.179), channel_id=1, source_target_pairs={{0,15},{1,0},{2,1},{3,2},{4,3},{5,4},{6,5},{7,6},{8,7},{9,8},{10,9... | collective-permute-start | bytes 28311560 | tf_op jit(solution)/shard_map/while/body/eval_jaxpr/ppermute | solution.py:35
  2439.8 55.4 %collective-permute-start = (bf16[1536,1536]{1,0:T(8,128)(2,1)}, bf16[1536,1536]{1,0:T(8,128)(2,1)}, u32[]{:S(2)}, u32[]{:S(2)}) collective-permute-start(bf16[1536,1536]{1,0:T(8,128)(2,1)} %get-tuple-element.178), channel_id=1, source_target_pairs={{0,15},{1,0},{2,1},{3,2},{4,3},{5,4},{6,5},{7,6},{8,7},{9,8},{10,9... | collective-permute-start | bytes 14155784 | tf_op jit(solution)/shard_map/while/body/eval_jaxpr/ppermute | solution.py:34
  2443.6 152.7 %collective-permute-start.1 = (f32[1536,1536]{1,0:T(8,128)}, f32[1536,1536]{1,0:T(8,128)}, u32[]{:S(2)}, u32[]{:S(2)}) collective-permute-start(f32[1536,1536]{1,0:T(8,128)} %get-tuple-element.179), channel_id=1, source_target_pairs={{0,15},{1,0},{2,1},{3,2},{4,3},{5,4},{6,5},{7,6},{8,7},{9,8},{10,9... | collective-permute-start | bytes 28311560 | tf_op jit(solution)/shard_map/while/body/eval_jaxpr/ppermute | solution.py:35
  2610.7 143.9 %collective-permute-start.2 = (f32[1536,1536]{1,0:T(8,128)}, f32[1536,1536]{1,0:T(8,128)}, u32[]{:S(2)}, u32[]{:S(2)}) collective-permute-start(f32[1536,1536]{1,0:T(8,128)} %get-tuple-element.65), channel_id=1, source_target_pairs={{0,15},{1,0},{2,1},{3,2},{4,3},{5,4},{6,5},{7,6},{8,7},{9,8},{10,9... | collective-permute-start | bytes 28311560 | tf_op jit(solution)/shard_map/ppermute | solution.py:41
  (84 other events, 5887.7 us)
where the time goes:
time: 2770 us
  waiting for transfers between devices  1590 us (57%)
  matrix products  801 us (29%)
  blocking collectives  127 us (5%)
  loops' own time  82.2 us (3%)
  local copies, waits for them, and re-layouts  81.5 us (3%)
  starting transfers between devices  61.9 us (2%)
    ppermute x15, waiting for transfers between devices, step_fn(): txt_acc = lax.ppermute(txt_acc, axis_name, shift_pairs)  812 us
    ppermute x15, waiting for transfers between devices, step_fn(): txt_block = lax.ppermute(txt_block, axis_name, shift_pairs)  773 us
    dot_general x16, matrix products, block_terms(): jnp.einsum('id,jd->ij', img_local, txt_block, preferred_element_type=jnp....  335 us
    dot_general x16, matrix products, block_terms(): jnp.einsum('ij,jd->id', coef_bf16, txt_block, preferred_element_type=jnp....  263 us
    dot_general x16, matrix products, block_terms(): jnp.einsum('ij,id->jd', coef_bf16, img_local, preferred_element_type=jnp....  203 us
    psum x1, blocking collectives, per_device(): lax.psum(jnp.stack([final_state[2], final_state[3], final_state[4]]), axi...  127 us
    another operation x1, loops' own time, per_device(): final_state = lax.fori_loop(1, n_dev, step_fn, init_state)  82.2 us
    while x165, local copies, waits for them, and re-layouts  78.4 us
  transfers between devices with their start and end apart: 31, of which 30 were waited for; matrix products, arithmetic and copies ran while one was open for 24% of the time, Pallas kernels for 0%

commit v1 on v0

v1 whole, which is shorter than its diff:
```python
import functools
import jax
import jax.numpy as jnp
from jax import lax
from jax.experimental import pallas as pl
from jax.experimental.pallas import tpu as pltpu
from jax.sharding import PartitionSpec as P

LOG2E = 1.4426950408889634
LN2 = 0.6931471805599453
BM = 512
STRIP = 32
CHUNK = 512
LANES = 256


def panel_body(cfg, *refs):
    seg_chunks, seg_acc, pieces, tin_flags, diag, bn = cfg
    refs = list(refs)
    take = lambda n: [refs.pop(0) for _ in range(n)]
    nseg, npc = len(seg_chunks), len(pieces)
    (sc,) = take(1)
    (sin,) = take(1)
    imgs, txts = take(nseg), take(npc)
    tins = take(sum(tin_flags))
    iins = take(sum(seg_acc))
    (sums,) = take(1)
    tos, ios = take(npc), take(nseg)
    T, TO, I, A, S, C, CR, tsem, osem, fsem, isem, asem, wsem = refs
    starts = [sum(seg_chunks[:k]) for k in range(nseg + 1)]
    G = starts[-1]
    Q = sum(pieces)
    D = T.shape[1]
    nth = Q // bn
    offs = [sum(pieces[:k]) for k in range(npc)]
    s2_, b2 = sc[0], sc[1]

    def t_copy(j):
        return pltpu.make_async_copy(txts[j], T.at[pl.ds(offs[j], pieces[j])], tsem.at[j])

    def tin_copy(j, r):
        return pltpu.make_async_copy(r, TO.at[pl.ds(offs[j], pieces[j])], osem.at[j])

    runs = []
    for j in range(npc):
        lo = offs[j]
        while lo < offs[j] + pieces[j]:
            hi = min((lo // bn + 1) * bn, offs[j] + pieces[j])
            runs.append((j, lo, hi - lo))
            lo = hi

    def flush(n):
        for q, (j, lo, size) in enumerate(runs):
            if lo // bn == n:
                flush_copy(q).start()

    def flush_copy(q):
        j, lo, size = runs[q]
        return pltpu.make_async_copy(TO.at[pl.ds(lo, size)], tos[j].at[pl.ds(lo - offs[j], size)], fsem.at[q])

    def when_seg(g, fn):
        for k in range(nseg):
            if nseg == 1:
                fn(k)
            else:
                pl.when((g >= starts[k]) & (g < starts[k + 1]))(functools.partial(fn, k))

    acc_src = []
    q = 0
    for k in range(nseg):
        acc_src.append(iins[q] if seg_acc[k] else None)
        q += seg_acc[k]

    def fetch(g):
        def one(k):
            rows = pl.ds((g - starts[k]) * BM, BM)
            pltpu.make_async_copy(imgs[k].at[rows], I.at[g % 4], isem.at[g % 4]).start()
            if seg_acc[k]:
                pltpu.make_async_copy(acc_src[k].at[rows], A.at[g % 4], asem.at[g % 4]).start()

        when_seg(g, one)

    def wait_img(g):
        pltpu.make_async_copy(imgs[0].at[pl.ds(0, BM)], I.at[g % 4], isem.at[g % 4]).wait()

    def open_acc(g):
        def one(k):
            if seg_acc[k]:
                pltpu.make_async_copy(acc_src[k].at[pl.ds(0, BM)], A.at[g % 4], asem.at[g % 4]).wait()
            else:
                A[g % 4] = jnp.zeros((BM, D), jnp.float32)

        when_seg(g, one)

    def put(g):
        def one(k):
            pltpu.make_async_copy(A.at[g % 4], ios[k].at[pl.ds((g - starts[k]) * BM, BM)], wsem.at[g % 4]).start()

        when_seg(g, one)

    def wait_put(g):
        pltpu.make_async_copy(A.at[g % 4], ios[0].at[pl.ds(0, BM)], wsem.at[g % 4]).wait()

    for j in range(npc):
        t_copy(j).start()
    fetch(jnp.int32(0))
    q = 0
    for j in range(npc):
        if tin_flags[j]:
            tin_copy(j, tins[q]).start()
            q += 1
        else:
            TO[pl.ds(offs[j], pieces[j])] = jnp.zeros((pieces[j], D), jnp.float32)
    sums[...] = sin[...]
    for j in range(npc):
        t_copy(j).wait()

    def tile(n):
        return pl.ds(pl.multiple_of(n * bn, bn), bn)


    def s1(g, n):
        S[...] = lax.dot_general(I[g % 4], T[tile(n), :], (((1,), (1,)), ((), ())), preferred_element_type=jnp.float32)

    def s2_strip(g, n, r0, accs, z):
        rs = pl.ds(r0, STRIP)
        dot = S[rs, :]
        bias = b2
        if z is not None:
            bz = z + b2
            bias = jnp.concatenate([bz] * (STRIP // 8), axis=0)
            bias = jnp.concatenate([bias] * (bn // 128), axis=1)
        v = dot * s2_ + bias
        if diag:
            rows = g * BM + r0 + lax.broadcasted_iota(jnp.int32, (STRIP, bn), 0)
            cols = n * bn + lax.broadcasted_iota(jnp.int32, (STRIP, bn), 1)
            on = rows == cols
            v = jnp.where(on, -v, v)
        w = jnp.minimum(v, 120.0)
        e = jnp.exp2(w)
        r = 1.0 / (1.0 + e)
        c = e * r
        fix = (1.0 - r) - c
        lg = jnp.log2(r) - (v - w)
        if diag:
            c = jnp.where(on, -c, c)
        C[rs, :] = c.astype(jnp.bfloat16)
        for q, val in enumerate((lg, fix, c, c * dot)):
            for k in range(0, STRIP, 8):
                for d0 in range(0, bn, LANES):
                    accs[q] = accs[q] + val[k : k + 8, d0 : d0 + LANES]

    def s2(g, n, toks=None):
        accs = [jnp.zeros((8, LANES), jnp.float32)] * 4
        NS = BM // STRIP
        for i in range(NS):
            z = None
            if toks:
                z = toks[min(len(toks) - 1, i * len(toks) // NS)] * 0.0
            s2_strip(g, n, i * STRIP, accs, z)
        for q in range(4):
            sums[q] += accs[q]

    def s3(g, n, toks):
        for d0 in range(0, D, CHUNK):
            val = A[g % 4, :, pl.ds(d0, CHUNK)] + jnp.dot(CR[...], T[tile(n), pl.ds(d0, CHUNK)], preferred_element_type=jnp.float32)
            A[g % 4, :, pl.ds(d0, CHUNK)] = val
            toks.append(val[:8, :128])
        for d0 in range(0, D, CHUNK):
            val = TO[tile(n), pl.ds(d0, CHUNK)] + lax.dot_general(CR[...], I[g % 4, :, pl.ds(d0, CHUNK)], (((0,), (0,)), ((), ())), preferred_element_type=jnp.float32)
            TO[tile(n), pl.ds(d0, CHUNK)] = val
            toks.append(val[:8, :128])

    wait_img(jnp.int32(0))
    if G > 1:
        fetch(jnp.int32(1))
    s1(jnp.int32(0), 0)
    q = 0
    for j in range(npc):
        if tin_flags[j]:
            tin_copy(j, tins[q]).wait()
            q += 1

    def split(t):
        return t // nth, t % nth

    def unit(t, with3):
        g, h = split(t)
        gp, hp = split(t - 1)
        gq, hq = split(t - 2)

        @pl.when(h == 0)
        def _():
            wait_img(g)

            @pl.when(g >= 3)
            def _():
                wait_put(g - 3)

            @pl.when(g + 1 < G)
            def _():
                fetch(g + 1)

        if with3:
            @pl.when(hq == 0)
            def _():
                open_acc(gq)

        toks = []
        if with3:
            CR[...] = C[...]
            s3(gq, hq, toks)
        s2(gp, hp, toks)
        s1(g, h)
        if with3:
            @pl.when(hq == nth - 1)
            def _():
                put(gq)

    unit(jnp.int32(1), False)

    def body(t, carry):
        unit(t, True)
        return carry

    NU = G * nth
    lax.fori_loop(2, NU, body, 0)
    gl = jnp.int32(G - 1)
    ga, ha = (NU - 2) // nth, (NU - 2) % nth
    if ha == 0:
        open_acc(jnp.int32(ga))
    for n in range(nth - 2):
        flush(n)
    CR[...] = C[...]
    toks = []
    s3(jnp.int32(ga), ha, toks)
    s2(gl, nth - 1, toks)
    if ha == nth - 1:
        put(jnp.int32(ga))
    else:
        flush(nth - 2)
    if nth == 1:
        open_acc(gl)
    CR[...] = C[...]
    s3(gl, nth - 1, [])
    put(gl)
    flush(nth - 1)
    for g in range(max(0, G - 3), G):
        wait_put(jnp.int32(g))
    for q in range(len(runs)):
        flush_copy(q).wait()


def panel(sc, sums, imgs, iins, txts, tins, diag=False, bn=512):
    return panel_call(sc, sums, imgs, iins, txts, tins, diag, bn)


def panel_call(sc, sums, imgs, iins, txts, tins, diag, bn):
    D = imgs[0].shape[1]
    cfg = (tuple(a.shape[0] // BM for a in imgs), tuple(a is not None for a in iins), tuple(a.shape[0] for a in txts), tuple(a is not None for a in tins), diag, bn)
    M, Q = sum(a.shape[0] for a in imgs), sum(a.shape[0] for a in txts)
    hbm = pl.BlockSpec(memory_space=pl.ANY)
    args = [sc, sums, *imgs, *txts, *[a for a in tins if a is not None]]
    na = len(args)
    ia = [a for a in iins if a is not None]
    args += ia
    out_shape = [jax.ShapeDtypeStruct(sums.shape, jnp.float32)]
    out_shape += [jax.ShapeDtypeStruct(a.shape, jnp.float32) for a in txts] + [jax.ShapeDtypeStruct(a.shape, jnp.float32) for a in imgs]
    alias = {}
    q = na
    for k, a in enumerate(iins):
        if a is not None:
            alias[q] = 1 + len(txts) + k
            q += 1
    in_specs = [pl.BlockSpec(memory_space=pltpu.SMEM), pl.BlockSpec(memory_space=pltpu.VMEM)] + [hbm] * (len(args) - 2)
    out_specs = [pl.BlockSpec(memory_space=pltpu.VMEM)] + [hbm] * (len(out_shape) - 1)
    outs = pl.pallas_call(
        functools.partial(panel_body, cfg),
        out_shape=out_shape,
        in_specs=in_specs,
        out_specs=out_specs,
        input_output_aliases=alias,
        scratch_shapes=[
            pltpu.VMEM((Q, D), jnp.bfloat16),
            pltpu.VMEM((Q, D), jnp.float32),
            pltpu.VMEM((4, BM, D), jnp.bfloat16),
            pltpu.VMEM((4, BM, D), jnp.float32),
            pltpu.VMEM((BM, bn), jnp.float32),
            pltpu.VMEM((BM, bn), jnp.bfloat16),
            pltpu.VMEM((BM, bn), jnp.bfloat16),
            pltpu.SemaphoreType.DMA((len(txts),)),
            pltpu.SemaphoreType.DMA((len(txts),)),
            pltpu.SemaphoreType.DMA((Q // bn + len(txts),)),
            pltpu.SemaphoreType.DMA((4,)),
            pltpu.SemaphoreType.DMA((4,)),
            pltpu.SemaphoreType.DMA((4,)),
        ],
        cost_estimate=pl.CostEstimate(flops=6 * M * Q * D, bytes_accessed=10 * M * D, transcendentals=3 * M * Q),
        compiler_params=pltpu.CompilerParams(vmem_limit_bytes=58 * 1024 * 1024),
        name="panel",
    )(*args)
    return outs[0], list(outs[1 : 1 + len(txts)]), list(outs[1 + len(txts) :])


def combine_body(starts, factor, base, *refs):
    refs = list(refs)
    out = refs.pop()
    g = pl.program_id(0)
    out[...] = base[...]
    for ref, (lo, hi) in zip(refs, starts):
        @pl.when((g >= lo) & (g < hi))
        def _():
            out[...] += ref[...]

    out[...] *= factor[0]


def combine_call(factor, base, groups):
    rows, D = base.shape
    br = 256
    starts, specs, args = [], [], []
    for group in groups:
        lo = 0
        for piece in group:
            n = piece.shape[0] // br
            starts.append((lo, lo + n))
            specs.append(pl.BlockSpec((br, D), functools.partial(lambda lo, n, g: (jnp.clip(g - lo, 0, n - 1), 0), lo, n)))
            args.append(piece)
            lo += n
    row = pl.BlockSpec((br, D), lambda g: (g, 0))
    return pl.pallas_call(
        functools.partial(combine_body, tuple(starts)),
        grid=(rows // br,),
        out_shape=jax.ShapeDtypeStruct(base.shape, jnp.float32),
        in_specs=[pl.BlockSpec(memory_space=pltpu.SMEM), row, *specs],
        out_specs=row,
        compiler_params=pltpu.CompilerParams(vmem_limit_bytes=32 * 1024 * 1024),
        cost_estimate=pl.CostEstimate(flops=rows * D * 64, bytes_accessed=16 * rows * D, transcendentals=0),
        name="combine",
    )(factor.reshape(1), base, *args)


def add_tail_body(factor, base, piece, out):
    out[...] = base[...] + piece[...] * factor[0]


def add_tail(factor, base, piece):
    rows, D = base.shape
    br = 256
    n = piece.shape[0] // br
    lo = rows // br - n
    late = pl.BlockSpec((br, D), lambda g: (lo + g, 0))
    return pl.pallas_call(
        add_tail_body,
        grid=(n,),
        out_shape=jax.ShapeDtypeStruct(base.shape, jnp.float32),
        in_specs=[pl.BlockSpec(memory_space=pltpu.SMEM), late, pl.BlockSpec((br, D), lambda g: (g, 0))],
        out_specs=late,
        input_output_aliases={1: 0},
        compiler_params=pltpu.CompilerParams(vmem_limit_bytes=32 * 1024 * 1024),
        name="add_tail",
    )(factor.reshape(1), base, piece)


def solution(mesh):
    axis = mesh.axis_names[0]
    n_dev = mesh.shape[axis]

    def swap(a, mask):
        return lax.ppermute(a, axis, [(i, i ^ mask) for i in range(n_dev)])

    CORE, X, Y, Z = 1, 2, 4, 8

    def step(img, txt, log_temp, logit_bias):
        rows = img.shape[0]
        n_total = rows * n_dev
        scale = jnp.exp(log_temp[0])
        sc = jnp.stack([scale * LOG2E, logit_bias[0] * LOG2E])
        sums = jnp.zeros((4, 8, LANES), jnp.float32)
        ha, hb = slice(0, rows // 2), slice(rows // 2, rows)
        x_cut = rows * 2 // 3

        img_c = swap(img, CORE)
        x0 = swap(img[:x_cut], X)
        x1 = swap(img[x_cut:], X)
        xc0 = swap(x0, CORE)
        xc1 = swap(x1, CORE)
        ya = swap(txt[ha], Y)
        zb = swap(txt[hb], Z)
        yza = swap(ya, Z)
        yzb = swap(zb, Y)
        yb = swap(txt[hb], Y)
        za = swap(txt[ha], Z)

        OC, X0, X1 = [img, img_c], [x0, xc0], [x1, xc1]
        N2 = [None, None]

        sums, own, oc = panel(sc, sums, OC, N2, [txt], [None], diag=True)
        sums, own, ax0 = panel(sc, sums, X0, N2, [txt], own)
        sums, p_yz, accs = panel(sc, sums, OC + X0 + X1, oc + ax0 + N2, [yza, yzb], N2)
        ry, rz = swap(p_yz[0], Z), swap(p_yz[1], Y)
        sums, p_zayb, accs = panel(sc, sums, OC + X0 + X1, accs, [za, yb], N2)
        oc, ax0, ax1 = accs[0:2], accs[2:4], accs[4:6]
        fz, fy = swap(p_zayb[0], Z), swap(p_zayb[1], Y)
        sums, p_yazb, ax0 = panel(sc, sums, X0, ax0, [ya, zb], [ry, rz])
        gx0 = swap(ax0[0] + swap(ax0[1], CORE), X)
        sums, p_yazb, accs = panel(sc, sums, OC + X1, oc + ax1, [ya, zb], p_yazb)
        oc, ax1 = accs[0:2], accs[2:4]
        gy, gz = swap(p_yazb[0], Y), swap(p_yazb[1], Z)
        gc = swap(oc[1], CORE)
        sums, own, ax1 = panel(sc, sums, X1, ax1, [txt], own)
        gx1 = swap(ax1[0] + swap(ax1[1], CORE), X)

        factor = scale / n_total
        txt_pre = combine_call(jnp.ones((), jnp.float32), own[0], [[fz, fy]])
        img_pre = combine_call(factor, oc[0], [[gc], [gx0]])
        txt_grad = combine_call(factor, txt_pre, [[gy, gz]])
        img_grad = add_tail(factor, img_pre, gx1)
        tot = jnp.sum(sums, axis=(1, 2))
        for mask in (CORE, Y, Z, X):
            tot = tot + swap(tot, mask)
        loss = -(tot[0:1] * LN2 + tot[1:2]) / n_total
        return loss, img_grad, txt_grad, tot[3:4] * factor, tot[2:3] / n_total

    split = P(axis, None)
    return jax.shard_map(step, mesh=mesh, in_specs=(split, split, P(None), P(None)), out_specs=(P(None), split, split, P(None), P(None)), check_vma=False)
```

time: 2770 us -> 926 us (0.33)
  waiting for transfers between devices: 1590 us -> 381 us
  matrix products: 801 us -> 0 us
  Pallas kernels: 0 us -> 479 us
  blocking collectives: 127 us -> 0 us
  loops' own time: 82.2 us -> 0 us
  local copies, waits for them, and re-layouts: 81.5 us -> 15 us
  starting transfers between devices: 61.9 us -> 26 us
    ppermute x31 -> x26, waiting for transfers between devices: 1590 us -> 381 us  [swap(): return lax.ppermute(a, axis, [(i, i ^ mask) for i in range(n_dev)])]
    dot_general x48 -> x0, matrix products: 801 us -> none  [the longest x16 335 us: block_terms(): jnp.einsum('id,jd->ij', img_local, txt_block, preferred_element_type=jnp....]
    pallas_call x0 -> x11, Pallas kernels: none -> 479 us  [the longest x7 452 us: panel_call(): pl.pallas_call(functools.partial(panel_body, cfg), out_shape=out_shape, i...]
    psum x1 -> x0, blocking collectives: 127 us -> none  [per_device(): lax.psum(jnp.stack([final_state[2], final_state[3], final_state[4]]), axi...]
    another operation x1 -> x0, loops' own time: 82.2 us -> none  [per_device(): final_state = lax.fori_loop(1, n_dev, step_fn, init_state)]
    while x165 -> x0, local copies, waits for them, and re-layouts: 78.4 us -> none
    ppermute x31 -> x26, starting transfers between devices: 61.9 us -> 26 us  [swap(): return lax.ppermute(a, axis, [(i, i ^ mask) for i in range(n_dev)])]
  transfers between devices with their start and end apart: 31 -> 26, of which waited for: 30 -> 8; matrix products, arithmetic and copies ran while one was open for 24% -> 2% of each run, Pallas kernels for 0% -> 52%
where the time goes in v1:
time: 926 us; the launch traced here: 922 us
  Pallas kernels  479 us (52%)
  waiting for transfers between devices  381 us (41%)
  starting transfers between devices  26 us (3%)
  local copies, waits for them, and re-layouts  15 us (2%)
  other arithmetic  12.5 us (1%)
    pallas_call x7, Pallas kernels, panel_call(): pl.pallas_call(functools.partial(panel_body, cfg), out_shape=out_shape, i...  452 us
    ppermute x26, waiting for transfers between devices, swap(): return lax.ppermute(a, axis, [(i, i ^ mask) for i in range(n_dev)])  381 us
    ppermute x26, starting transfers between devices, swap(): return lax.ppermute(a, axis, [(i, i ^ mask) for i in range(n_dev)])  26 us
    pallas_call x3, Pallas kernels, combine_call(): pl.pallas_call(functools.partial(combine_body, tuple(starts)), grid=(rows...  22.9 us
  transfers between devices with their start and end apart: 26, of which 8 were waited for; matrix products, arithmetic and copies ran while one was open for 2% of the time, Pallas kernels for 52%

profile of v1, /device:TPU:0, one launch (start us, length us, event | category | flops | bytes accessed | tf_op | source)
XLA Modules:
  0.0 922.3 jit_solution(3987038796237770127)
XLA Ops:
  1.4 2.5 slice.26
  3.9 2.3 collective-permute-start.1
  6.2 2.5 fusion
  16.2 58.9 %collective-permute-done.1.refs_2_.refs_4_ = bf16[1024,1536]{1,0:T(8,128)(2,1)S(1)} collective-permute-done((bf16[1024,1536]{1,0:T(8,128)(2,1)S(1)}, bf16[1024,1536]{1,0:T(8,128)(2,1)S(1)}, u32[]{:S(2)}, u32[]{:S(2)}) %collective-permute-start.1) | collective-permute-done | bytes 3145760 | tf_op jit(solution)/shard_map/ppermute | solution.py:370
  77.8 57.0 %panel.7 = (f32[4,8,256]{2,1,0:T(8,128)}, f32[1536,1536]{1,0:T(8,128)}, f32[1536,1536]{1,0:T(8,128)}, f32[1536,1536]{1,0:T(8,128)}) custom-call(f32[2]{0:T(128)} %pad_maximum_fusion.refs_0_, f32[4,8,256]{2,1,0:T(8,128)} %broadcast_in_dim.3.refs_1_, bf16[1536,1536]{1,0:T(8,128)(2,1)} %refs_2_.7, bf16[1536,1536]{1,0:T(8,128)(2,1)} %collective-permute-done.refs_3_, ...), custom_call_target="tpu_custom_call" | custom-call | flops 43486543872 | bytes 47185920 | tf_op jit(solution)/shard_map/panel/pallas_call | solution.py:277
  137.5 42.6 %panel.8 = (f32[4,8,256]{2,1,0:T(8,128)}, f32[1536,1536]{1,0:T(8,128)}, f32[1024,1536]{1,0:T(8,128)}, f32[1024,1536]{1,0:T(8,128)}) custom-call(f32[2]{0:T(128)} %pad_maximum_fusion.refs_0_, f32[4,8,256]{2,1,0:T(8,128)} %get-tuple-element.47.refs_1_, bf16[1024,1536]{1,0:T(8,128)(2,1)} %copy-done.4, ...), custom_call_target="tpu_custom_call" | custom-call | flops 28991029248 | bytes 31457280 | tf_op jit(solution)/shard_map/panel/pallas_call | solution.py:277
  180.1 10.3 %collective-permute-done.8.refs_9_ = bf16[768,1536]{1,0:T(8,128)(2,1)} collective-permute-done((bf16[768,1536]{1,0:T(8,128)(2,1)}, bf16[768,1536]{1,0:T(8,128)(2,1)}, u32[]{:S(2)}, u32[]{:S(2)}) %collective-permute-start.8) | collective-permute-done | bytes 2359328 | tf_op jit(solution)/shard_map/ppermute | solution.py:370
  190.4 48.9 %collective-permute-done.6.refs_8_ = bf16[768,1536]{1,0:T(8,128)(2,1)S(1)} collective-permute-done((bf16[768,1536]{1,0:T(8,128)(2,1)}, bf16[768,1536]{1,0:T(8,128)(2,1)S(1)}, u32[]{:S(2)}, u32[]{:S(2)}) %collective-permute-start.6) | collective-permute-done | bytes 2359328 | tf_op jit(solution)/shard_map/ppermute | solution.py:370
  240.7 104.8 %panel.9 = (f32[4,8,256]{2,1,0:T(8,128)}, f32[768,1536]{1,0:T(8,128)}, f32[768,1536]{1,0:T(8,128)}, f32[1536,1536]{1,0:T(8,128)}, f32[1536,1536]{1,0:T(8,128)}, ...) custom-call(f32[2]{0:T(128)} %pad_maximum_fusion.refs_0_, ...), custom_call_target="tpu_custom_call", output_to_operand_aliasing={{3}: (10, {}), {4}: (11, {}), {5}: (12, {}), {6}: (13, {})} | custom-call | flops 86973087744 | bytes 94371840 | tf_op jit(solution)/shard_map/panel/pallas_call | solution.py:277
  347.6 104.6 %panel.10 = (f32[4,8,256]{2,1,0:T(8,128)}, f32[768,1536]{1,0:T(8,128)}, f32[768,1536]{1,0:T(8,128)}, f32[1536,1536]{1,0:T(8,128)}, f32[1536,1536]{1,0:T(8,128)},...) custom-call(f32[2]{0:T(128)} %pad_maximum_fusion.refs_0_, ...), custom_call_target="tpu_custom_call", output_to_operand_aliasing={{3}: (10, {}), {4}: (11, {}), {5}: (12, {}), {6}: (13, {}),... | custom-call | flops 86973087744 | bytes 94371840 | tf_op jit(solution)/shard_map/panel/pallas_call | solution.py:277
  454.7 42.5 %panel.11 = (f32[4,8,256]{2,1,0:T(8,128)}, f32[768,1536]{1,0:T(8,128)}, f32[768,1536]{1,0:T(8,128)}, f32[1024,1536]{1,0:T(8,128)}, f32[1024,1536]{1,0:T(8,128)}) custom-call(f32[2]{0:T(128)} %pad_maximum_fusion.refs_0_, f32[4,8,256]{2,1,0:T(8,128)} %get-tuple-element.61.refs_1_, ...), custom_call_target="tpu_custom_call", output_to_operand_aliasing={{3}: (8, {}), {4}: (9, {})} | custom-call | flops 28991029248 | bytes 31457280 | tf_op jit(solution)/shard_map/panel/pallas_call | solution.py:277
  497.2 74.3 %panel.12 = (f32[4,8,256]{2,1,0:T(8,128)}, f32[768,1536]{1,0:T(8,128)}, f32[768,1536]{1,0:T(8,128)}, f32[1536,1536]{1,0:T(8,128)}, f32[1536,1536]{1,0:T(8,128)},...) custom-call(f32[2]{0:T(128)} %pad_maximum_fusion.refs_0_, ...), custom_call_target="tpu_custom_call", output_to_operand_aliasing={{3}: (10, {}), {4}: (11, {}), {5}: (12, {}), {6}: (13, {})} | custom-call | flops 57982058496 | bytes 62914560 | tf_op jit(solution)/shard_map/panel/pallas_call | solution.py:277
  572.1 26.8 %panel.13 = (f32[4,8,256]{2,1,0:T(8,128)}, f32[1536,1536]{1,0:T(8,128)}, f32[512,1536]{1,0:T(8,128)}, f32[512,1536]{1,0:T(8,128)}) custom-call(f32[2]{0:T(128)} %pad_maximum_fusion.refs_0_, f32[4,8,256]{2,1,0:T(8,128)} %get-tuple-element.73.refs_1_, ...), custom_call_target="tpu_custom_call", output_to_operand_aliasing={{2}: (6, {}), {3}: (7, {})} | custom-call | flops 14495514624 | bytes 15728640 | tf_op jit(solution)/shard_map/panel/pallas_call | solution.py:277
  600.3 4.5 collective-permute-done.13
  606.8 8.8 add.26
  615.5 93.3 %collective-permute-done.14 = f32[4]{0:T(128)S(1)} collective-permute-done((f32[4]{0:T(128)S(1)}, f32[4]{0:T(128)S(1)}, u32[]{:S(2)}, u32[]{:S(2)}) %collective-permute-start.14) | collective-permute-done | bytes 48 | tf_op jit(solution)/shard_map/ppermute | solution.py:370
  717.2 2.3 add.27
  720.0 125.8 %collective-permute-done.16 = f32[4]{0:T(128)S(1)} collective-permute-done((f32[4]{0:T(128)S(1)}, f32[4]{0:T(128)S(1)}, u32[]{:S(2)}, u32[]{:S(2)}) %collective-permute-start.16) | collective-permute-done | bytes 48 | tf_op jit(solution)/shard_map/ppermute | solution.py:370
  847.5 7.2 combine.4.base
  857.9 5.1 combine.5
  863.0 3.7 copy-done
  866.6 10.6 %combine.3.base = f32[1536,1536]{1,0:T(8,128)} custom-call(f32[1]{0:T(128)S(6)} %div.10.factor, f32[1536,1536]{1,0:T(8,128)S(1)} %copy-done, f32[1536,1536]{1,0:T(8,128)} %collective-permute-done.17.refs_0_, f32[1024,1536]{1,0:T(8,128)} %collective-permute-done.19.refs_1_), custom_call_target="tpu_custom_call" | custom-call | flops 150994944 | bytes 37748736 | tf_op jit(solution)/shard_map/combine/pallas_call | solution.py:331
  877.3 37.2 %collective-permute-done.21.piece = f32[512,1536]{1,0:T(8,128)} collective-permute-done((f32[512,1536]{1,0:T(8,128)}, f32[512,1536]{1,0:T(8,128)}, u32[]{:S(2)}, u32[]{:S(2)}) %collective-permute-start.21) | collective-permute-done | bytes 3145760 | tf_op jit(solution)/shard_map/ppermute | solution.py:370
  914.5 4.1 add_tail.1
  (64 shorter events, 33.5 us)
Async XLA Ops:
  0.6 76.5 %collective-permute-start = (bf16[1536,1536]{1,0:T(8,128)(2,1)}, bf16[1536,1536]{1,0:T(8,128)(2,1)}, u32[]{:S(2)}, u32[]{:S(2)}) collective-permute-start(bf16[1536,1536]{1,0:T(8,128)(2,1)} %refs_2_.7), channel_id=1, source_target_pairs={{0,1},{1,0},{2,3},{3,2},{4,5},{5,4},{6,7},{7,6},{8,9},{9,8},{10,11... | collective-permute-start | bytes 14155784 | tf_op jit(solution)/shard_map/ppermute | solution.py:370
  3.9 71.3 %collective-permute-start.1 = (bf16[1024,1536]{1,0:T(8,128)(2,1)S(1)}, bf16[1024,1536]{1,0:T(8,128)(2,1)S(1)}, u32[]{:S(2)}, u32[]{:S(2)}) collective-permute-start(bf16[1024,1536]{1,0:T(8,128)(2,1)S(1)} %slice.26), channel_id=1, source_target_pairs={{0,2},{1,3},{2,0},{3,1},{4,6},{5,7},{6,4},{7,5},{8,10},{9,11},{10,... | collective-permute-start | bytes 9437192 | tf_op jit(solution)/shard_map/ppermute | solution.py:370
  8.7 338.9 %collective-permute-start.10 = (bf16[768,1536]{1,0:T(8,128)(2,1)}, bf16[768,1536]{1,0:T(8,128)(2,1)}, u32[]{:S(2)}, u32[]{:S(2)}) collective-permute-start(bf16[768,1536]{1,0:T(8,128)(2,1)} %get-tuple-element.89), channel_id=1, source_target_pairs={{0,4},{1,5},{2,6},{3,7},{4,0},{5,1},{6,2},{7,3},{8,12},{9,13},{10,... | collective-permute-start | bytes 7077896 | tf_op jit(solution)/shard_map/ppermute | solution.py:370
  10.2 126.2 %collective-permute-start.7 = (bf16[768,1536]{1,0:T(8,128)(2,1)}, bf16[768,1536]{1,0:T(8,128)(2,1)}, u32[]{:S(2)}, u32[]{:S(2)}) collective-permute-start(bf16[768,1536]{1,0:T(8,128)(2,1)} %get-tuple-element.89), channel_id=1, source_target_pairs={{0,8},{1,9},{2,10},{3,11},{4,12},{5,13},{6,14},{7,15},{8,0},{9,1},... | collective-permute-start | bytes 7077896 | tf_op jit(solution)/shard_map/ppermute | solution.py:370
  13.3 121.5 %collective-permute-start.3 = (bf16[512,1536]{1,0:T(8,128)(2,1)S(1)}, bf16[512,1536]{1,0:T(8,128)(2,1)}, u32[]{:S(2)}, u32[]{:S(2)}) collective-permute-start(bf16[512,1536]{1,0:T(8,128)(2,1)S(1)} %slice.27), channel_id=1, source_target_pairs={{0,2},{1,3},{2,0},{3,1},{4,6},{5,7},{6,4},{7,5},{8,10},{9,11},{10,... | collective-permute-start | bytes 4718600 | tf_op jit(solution)/shard_map/ppermute | solution.py:370
  75.1 61.5 %collective-permute-start.5 = (bf16[768,1536]{1,0:T(8,128)(2,1)}, bf16[768,1536]{1,0:T(8,128)(2,1)}, u32[]{:S(2)}, u32[]{:S(2)}) collective-permute-start(bf16[768,1536]{1,0:T(8,128)(2,1)} %get-tuple-element.90), channel_id=1, source_target_pairs={{0,4},{1,5},{2,6},{3,7},{4,0},{5,1},{6,2},{7,3},{8,12},{9,13},{10,... | collective-permute-start | bytes 7077896 | tf_op jit(solution)/shard_map/ppermute | solution.py:370
  77.2 60.1 %collective-permute-start.2 = (bf16[1024,1536]{1,0:T(8,128)(2,1)S(1)}, bf16[1024,1536]{1,0:T(8,128)(2,1)}, u32[]{:S(2)}, u32[]{:S(2)}) collective-permute-start(bf16[1024,1536]{1,0:T(8,128)(2,1)S(1)} %collective-permute-done.1.refs_2_.refs_4_), channel_id=1, source_target_pairs={{0,1},{1,0},{2,3},{3,2},{4,5},{5,4},{6,7},{7,6},{8,9},{9,8},{10,11... | collective-permute-start | bytes 9437192 | tf_op jit(solution)/shard_map/ppermute | solution.py:370
  134.8 212.8 %collective-permute-start.9 = (bf16[768,1536]{1,0:T(8,128)(2,1)}, bf16[768,1536]{1,0:T(8,128)(2,1)}, u32[]{:S(2)}, u32[]{:S(2)}) collective-permute-start(bf16[768,1536]{1,0:T(8,128)(2,1)} %get-tuple-element.90), channel_id=1, source_target_pairs={{0,8},{1,9},{2,10},{3,11},{4,12},{5,13},{6,14},{7,15},{8,0},{9,1},... | collective-permute-start | bytes 7077896 | tf_op jit(solution)/shard_map/ppermute | solution.py:370
  136.4 43.7 %collective-permute-start.4 = (bf16[512,1536]{1,0:T(8,128)(2,1)}, bf16[512,1536]{1,0:T(8,128)(2,1)}, u32[]{:S(2)}, u32[]{:S(2)}) collective-permute-start(bf16[512,1536]{1,0:T(8,128)(2,1)} %collective-permute-done.3.refs_6_.refs_4_.refs_2_), channel_id=1, source_target_pairs={{0,1},{1,0},{2,3},{3,2},{4,5},{5,4},{6,7},{7,6},{8,9},{9,8},{10,11... | collective-permute-start | bytes 4718600 | tf_op jit(solution)/shard_map/ppermute | solution.py:370
  136.6 53.8 %collective-permute-start.8 = (bf16[768,1536]{1,0:T(8,128)(2,1)}, bf16[768,1536]{1,0:T(8,128)(2,1)}, u32[]{:S(2)}, u32[]{:S(2)}) collective-permute-start(bf16[768,1536]{1,0:T(8,128)(2,1)} %collective-permute-done.7.refs_5_.refs_7_), channel_id=1, source_target_pairs={{0,4},{1,5},{2,6},{3,7},{4,0},{5,1},{6,2},{7,3},{8,12},{9,13},{10,... | collective-permute-start | bytes 7077896 | tf_op jit(solution)/shard_map/ppermute | solution.py:370
  137.3 101.9 %collective-permute-start.6 = (bf16[768,1536]{1,0:T(8,128)(2,1)}, bf16[768,1536]{1,0:T(8,128)(2,1)S(1)}, u32[]{:S(2)}, u32[]{:S(2)}) collective-permute-start(bf16[768,1536]{1,0:T(8,128)(2,1)} %collective-permute-done.5.refs_4_.refs_6_), channel_id=1, source_target_pairs={{0,8},{1,9},{2,10},{3,11},{4,12},{5,13},{6,14},{7,15},{8,0},{9,1},... | collective-permute-start | bytes 7077896 | tf_op jit(solution)/shard_map/ppermute | solution.py:370
  345.4 107.0 %collective-permute-start.11 = (f32[768,1536]{1,0:T(8,128)}, f32[768,1536]{1,0:T(8,128)S(1)}, u32[]{:S(2)}, u32[]{:S(2)}) collective-permute-start(f32[768,1536]{1,0:T(8,128)} %get-tuple-element.62), channel_id=1, source_target_pairs={{0,8},{1,9},{2,10},{3,11},{4,12},{5,13},{6,14},{7,15},{8,0},{9,1},... | collective-permute-start | bytes 14155784 | tf_op jit(solution)/shard_map/ppermute | solution.py:370
  347.1 105.4 %collective-permute-start.12 = (f32[768,1536]{1,0:T(8,128)}, f32[768,1536]{1,0:T(8,128)}, u32[]{:S(2)}, u32[]{:S(2)}) collective-permute-start(f32[768,1536]{1,0:T(8,128)} %get-tuple-element.63), channel_id=1, source_target_pairs={{0,4},{1,5},{2,6},{3,7},{4,0},{5,1},{6,2},{7,3},{8,12},{9,13},{10,... | collective-permute-start | bytes 14155784 | tf_op jit(solution)/shard_map/ppermute | solution.py:370
  452.2 258.4 %collective-permute-start.22 = (f32[768,1536]{1,0:T(8,128)}, f32[768,1536]{1,0:T(8,128)}, u32[]{:S(2)}, u32[]{:S(2)}) collective-permute-start(f32[768,1536]{1,0:T(8,128)} %get-tuple-element.85), channel_id=1, source_target_pairs={{0,8},{1,9},{2,10},{3,11},{4,12},{5,13},{6,14},{7,15},{8,0},{9,1},... | collective-permute-start | bytes 14155784 | tf_op jit(solution)/shard_map/ppermute | solution.py:370
  497.2 109.2 %collective-permute-start.18 = (f32[1024,1536]{1,0:T(8,128)}, f32[1024,1536]{1,0:T(8,128)}, u32[]{:S(2)}, u32[]{:S(2)}) collective-permute-start(f32[1024,1536]{1,0:T(8,128)} %get-tuple-element.81), channel_id=1, source_target_pairs={{0,1},{1,0},{2,3},{3,2},{4,5},{5,4},{6,7},{7,6},{8,9},{9,8},{10,11... | collective-permute-start | bytes 18874376 | tf_op jit(solution)/shard_map/ppermute | solution.py:370
  571.5 291.4 %collective-permute-start.17 = (f32[1536,1536]{1,0:T(8,128)}, f32[1536,1536]{1,0:T(8,128)}, u32[]{:S(2)}, u32[]{:S(2)}) collective-permute-start(f32[1536,1536]{1,0:T(8,128)} %get-tuple-element.79), channel_id=1, source_target_pairs={{0,1},{1,0},{2,3},{3,2},{4,5},{5,4},{6,7},{7,6},{8,9},{9,8},{10,11... | collective-permute-start | bytes 28311560 | tf_op jit(solution)/shard_map/ppermute | solution.py:370
  598.8 116.8 %collective-permute-start.20 = (f32[512,1536]{1,0:T(8,128)}, f32[512,1536]{1,0:T(8,128)S(1)}, u32[]{:S(2)}, u32[]{:S(2)}) collective-permute-start(f32[512,1536]{1,0:T(8,128)} %get-tuple-element.83), channel_id=1, source_target_pairs={{0,1},{1,0},{2,3},{3,2},{4,5},{5,4},{6,7},{7,6},{8,9},{9,8},{10,11... | collective-permute-start | bytes 9437192 | tf_op jit(solution)/shard_map/ppermute | solution.py:370
  604.7 114.8 %collective-permute-start.23 = (f32[768,1536]{1,0:T(8,128)}, f32[768,1536]{1,0:T(8,128)S(1)}, u32[]{:S(2)}, u32[]{:S(2)}) collective-permute-start(f32[768,1536]{1,0:T(8,128)} %get-tuple-element.86), channel_id=1, source_target_pairs={{0,4},{1,5},{2,6},{3,7},{4,0},{5,1},{6,2},{7,3},{8,12},{9,13},{10,... | collective-permute-start | bytes 14155784 | tf_op jit(solution)/shard_map/ppermute | solution.py:370
  606.4 102.5 %collective-permute-start.14 = (f32[4]{0:T(128)S(1)}, f32[4]{0:T(128)S(1)}, u32[]{:S(2)}, u32[]{:S(2)}) collective-permute-start(f32[4]{0:T(128)S(1)} %add.21), channel_id=1, source_target_pairs={{0,4},{1,5},{2,6},{3,7},{4,0},{5,1},{6,2},{7,3},{8,12},{9,13},{10,... | collective-permute-start | bytes 56 | tf_op jit(solution)/shard_map/ppermute | solution.py:370
  708.9 154.1 %collective-permute-start.19 = (f32[1024,1536]{1,0:T(8,128)}, f32[1024,1536]{1,0:T(8,128)}, u32[]{:S(2)}, u32[]{:S(2)}) collective-permute-start(f32[1024,1536]{1,0:T(8,128)} %add.26), channel_id=1, source_target_pairs={{0,2},{1,3},{2,0},{3,1},{4,6},{5,7},{6,4},{7,5},{8,10},{9,11},{10,... | collective-permute-start | bytes 18874376 | tf_op jit(solution)/shard_map/ppermute | solution.py:370
  714.1 143.7 %collective-permute-start.24 = (f32[768,1536]{1,0:T(8,128)}, f32[768,1536]{1,0:T(8,128)S(1)}, u32[]{:S(2)}, u32[]{:S(2)}) collective-permute-start(f32[768,1536]{1,0:T(8,128)} %get-tuple-element.87), channel_id=1, source_target_pairs={{0,4},{1,5},{2,6},{3,7},{4,0},{5,1},{6,2},{7,3},{8,12},{9,13},{10,... | collective-permute-start | bytes 14155784 | tf_op jit(solution)/shard_map/ppermute | solution.py:370
  715.6 142.2 %collective-permute-start.25 = (f32[768,1536]{1,0:T(8,128)}, f32[768,1536]{1,0:T(8,128)S(1)}, u32[]{:S(2)}, u32[]{:S(2)}) collective-permute-start(f32[768,1536]{1,0:T(8,128)} %get-tuple-element.88), channel_id=1, source_target_pairs={{0,8},{1,9},{2,10},{3,11},{4,12},{5,13},{6,14},{7,15},{8,0},{9,1},... | collective-permute-start | bytes 14155784 | tf_op jit(solution)/shard_map/ppermute | solution.py:370
  719.5 126.3 %collective-permute-start.16 = (f32[4]{0:T(128)S(1)}, f32[4]{0:T(128)S(1)}, u32[]{:S(2)}, u32[]{:S(2)}) collective-permute-start(f32[4]{0:T(128)S(1)} %add.23), channel_id=1, source_target_pairs={{0,2},{1,3},{2,0},{3,1},{4,6},{5,7},{6,4},{7,5},{8,10},{9,11},{10,... | collective-permute-start | bytes 56 | tf_op jit(solution)/shard_map/ppermute | solution.py:370
  845.8 68.7 %collective-permute-start.21 = (f32[512,1536]{1,0:T(8,128)}, f32[512,1536]{1,0:T(8,128)}, u32[]{:S(2)}, u32[]{:S(2)}) collective-permute-start(f32[512,1536]{1,0:T(8,128)} %add.27), channel_id=1, source_target_pairs={{0,2},{1,3},{2,0},{3,1},{4,6},{5,7},{6,4},{7,5},{8,10},{9,11},{10,... | collective-permute-start | bytes 9437192 | tf_op jit(solution)/shard_map/ppermute | solution.py:370
  (8 other events, 191.5 us)

commit v2 on v1

--- a/solution.py
+++ b/solution.py
@@ -15,7 +15,7 @@
 
 
 def panel_body(cfg, *refs):
-    seg_chunks, seg_acc, pieces, tin_flags, diag, bn = cfg
+    seg_chunks, seg_acc, pieces, tin_flags, diag, bn, cuts = cfg
     refs = list(refs)
     take = lambda n: [refs.pop(0) for _ in range(n)]
     nseg, npc = len(seg_chunks), len(pieces)
@@ -25,38 +25,52 @@
     tins = take(sum(tin_flags))
     iins = take(sum(seg_acc))
     (sums,) = take(1)
-    tos, ios = take(npc), take(nseg)
+    tos, ios = take(len(cuts)), take(nseg)
     T, TO, I, A, S, C, CR, tsem, osem, fsem, isem, asem, wsem = refs
     starts = [sum(seg_chunks[:k]) for k in range(nseg + 1)]
     G = starts[-1]
     Q = sum(pieces)
     D = T.shape[1]
     nth = Q // bn
-    offs = [sum(pieces[:k]) for k in range(npc)]
     s2_, b2 = sc[0], sc[1]
 
-    def t_copy(j):
-        return pltpu.make_async_copy(txts[j], T.at[pl.ds(offs[j], pieces[j])], tsem.at[j])
-
-    def tin_copy(j, r):
-        return pltpu.make_async_copy(r, TO.at[pl.ds(offs[j], pieces[j])], osem.at[j])
-
-    runs = []
-    for j in range(npc):
-        lo = offs[j]
-        while lo < offs[j] + pieces[j]:
-            hi = min((lo // bn + 1) * bn, offs[j] + pieces[j])
-            runs.append((j, lo, hi - lo))
-            lo = hi
+    def cut_runs(sizes):
+        runs, at = [], 0
+        for j, size in enumerate(sizes):
+            lo = at
+            while lo < at + size:
+                hi = min((lo // bn + 1) * bn, at + size)
+                runs.append((j, lo, hi - lo, lo - at))
+                lo = hi
+            at += size
+        return runs
+
+    runs, out_runs = cut_runs(pieces), cut_runs(cuts)
+
+    def load_text(n):
+        for j, lo, size, at in runs:
+            if lo // bn == n:
+                pltpu.make_async_copy(txts[j].at[pl.ds(at, size)], T.at[pl.ds(lo, size)], tsem.at[n]).start()
+
+    def wait_text(n):
+        pltpu.make_async_copy(imgs[0].at[pl.ds(0, bn)], T.at[pl.ds(0, bn)], tsem.at[n]).wait()
+
+    def load_sum(n):
+        for j, lo, size, at in runs:
+            if lo // bn == n:
+                pltpu.make_async_copy(tins[j].at[pl.ds(at, size)], TO.at[pl.ds(lo, size)], osem.at[n]).start()
+
+    def wait_sum(n):
+        pltpu.make_async_copy(ios[0].at[pl.ds(0, bn)], TO.at[pl.ds(0, bn)], osem.at[n]).wait()
 
     def flush(n):
-        for q, (j, lo, size) in enumerate(runs):
-            if lo // bn == n:
+        for q, run in enumerate(out_runs):
+            if run[1] // bn == n:
                 flush_copy(q).start()
 
     def flush_copy(q):
-        j, lo, size = runs[q]
-        return pltpu.make_async_copy(TO.at[pl.ds(lo, size)], tos[j].at[pl.ds(lo - offs[j], size)], fsem.at[q])
+        j, lo, size, at = out_runs[q]
+        return pltpu.make_async_copy(TO.at[pl.ds(lo, size)], tos[j].at[pl.ds(at, size)], fsem.at[q])
 
     def when_seg(g, fn):
         for k in range(nseg):
@@ -101,19 +115,16 @@
     def wait_put(g):
         pltpu.make_async_copy(A.at[g % 4], ios[0].at[pl.ds(0, BM)], wsem.at[g % 4]).wait()
 
-    for j in range(npc):
-        t_copy(j).start()
+    load_text(0)
     fetch(jnp.int32(0))
-    q = 0
-    for j in range(npc):
-        if tin_flags[j]:
-            tin_copy(j, tins[q]).start()
-            q += 1
-        else:
-            TO[pl.ds(offs[j], pieces[j])] = jnp.zeros((pieces[j], D), jnp.float32)
+    for n in range(1, nth):
+        load_text(n)
+    if tins:
+        for n in range(nth):
+            load_sum(n)
+    else:
+        TO[...] = jnp.zeros((Q, D), jnp.float32)
     sums[...] = sin[...]
-    for j in range(npc):
-        t_copy(j).wait()
 
     def tile(n):
         return pl.ds(pl.multiple_of(n * bn, bn), bn)
@@ -162,24 +173,25 @@
             sums[q] += accs[q]
 
     def s3(g, n, toks):
+        s3_img(g, n, toks)
+        s3_txt(g, n, toks)
+
+    def s3_img(g, n, toks):
         for d0 in range(0, D, CHUNK):
             val = A[g % 4, :, pl.ds(d0, CHUNK)] + jnp.dot(CR[...], T[tile(n), pl.ds(d0, CHUNK)], preferred_element_type=jnp.float32)
             A[g % 4, :, pl.ds(d0, CHUNK)] = val
             toks.append(val[:8, :128])
+
+    def s3_txt(g, n, toks):
         for d0 in range(0, D, CHUNK):
             val = TO[tile(n), pl.ds(d0, CHUNK)] + lax.dot_general(CR[...], I[g % 4, :, pl.ds(d0, CHUNK)], (((0,), (0,)), ((), ())), preferred_element_type=jnp.float32)
             TO[tile(n), pl.ds(d0, CHUNK)] = val
             toks.append(val[:8, :128])
 
+    wait_text(0)
     wait_img(jnp.int32(0))
-    if G > 1:
-        fetch(jnp.int32(1))
+    fetch(jnp.int32(1))
     s1(jnp.int32(0), 0)
-    q = 0
-    for j in range(npc):
-        if tin_flags[j]:
-            tin_copy(j, tins[q]).wait()
-            q += 1
 
     def split(t):
         return t // nth, t % nth
@@ -205,6 +217,16 @@
             @pl.when(hq == 0)
             def _():
                 open_acc(gq)
+
+            if nth > 2:
+                @pl.when(g == 0)
+                def _():
+                    wait_text(h)
+
+            if tins:
+                @pl.when(gq == 0)
+                def _():
+                    wait_sum(hq)
 
         toks = []
         if with3:
@@ -217,6 +239,8 @@
             def _():
                 put(gq)
 
+    for n in range(1, min(nth, 2)):
+        wait_text(n)
     unit(jnp.int32(1), False)
 
     def body(t, carry):
@@ -242,22 +266,23 @@
     if nth == 1:
         open_acc(gl)
     CR[...] = C[...]
-    s3(gl, nth - 1, [])
+    s3_img(gl, nth - 1, [])
     put(gl)
+    s3_txt(gl, nth - 1, [])
     flush(nth - 1)
     for g in range(max(0, G - 3), G):
         wait_put(jnp.int32(g))
-    for q in range(len(runs)):
+    for q in range(len(out_runs)):
         flush_copy(q).wait()
 
 
-def panel(sc, sums, imgs, iins, txts, tins, diag=False, bn=512):
-    return panel_call(sc, sums, imgs, iins, txts, tins, diag, bn)
-
-
-def panel_call(sc, sums, imgs, iins, txts, tins, diag, bn):
+def panel(sc, sums, imgs, iins, txts, tins, diag=False, bn=512, cuts=None):
+    return panel_call(sc, sums, imgs, iins, txts, tins, diag, bn, cuts or tuple(a.shape[0] for a in txts))
+
+
+def panel_call(sc, sums, imgs, iins, txts, tins, diag, bn, cuts):
     D = imgs[0].shape[1]
-    cfg = (tuple(a.shape[0] // BM for a in imgs), tuple(a is not None for a in iins), tuple(a.shape[0] for a in txts), tuple(a is not None for a in tins), diag, bn)
+    cfg = (tuple(a.shape[0] // BM for a in imgs), tuple(a is not None for a in iins), tuple(a.shape[0] for a in txts), tuple(a is not None for a in tins), diag, bn, cuts)
     M, Q = sum(a.shape[0] for a in imgs), sum(a.shape[0] for a in txts)
     hbm = pl.BlockSpec(memory_space=pl.ANY)
     args = [sc, sums, *imgs, *txts, *[a for a in tins if a is not None]]
@@ -265,12 +290,12 @@
     ia = [a for a in iins if a is not None]
     args += ia
     out_shape = [jax.ShapeDtypeStruct(sums.shape, jnp.float32)]
-    out_shape += [jax.ShapeDtypeStruct(a.shape, jnp.float32) for a in txts] + [jax.ShapeDtypeStruct(a.shape, jnp.float32) for a in imgs]
+    out_shape += [jax.ShapeDtypeStruct((c, D), jnp.float32) for c in cuts] + [jax.ShapeDtypeStruct(a.shape, jnp.float32) for a in imgs]
     alias = {}
     q = na
     for k, a in enumerate(iins):
         if a is not None:
-            alias[q] = 1 + len(txts) + k
+            alias[q] = 1 + len(cuts) + k
             q += 1
     in_specs = [pl.BlockSpec(memory_space=pltpu.SMEM), pl.BlockSpec(memory_space=pltpu.VMEM)] + [hbm] * (len(args) - 2)
     out_specs = [pl.BlockSpec(memory_space=pltpu.VMEM)] + [hbm] * (len(out_shape) - 1)
@@ -288,9 +313,9 @@
             pltpu.VMEM((BM, bn), jnp.float32),
             pltpu.VMEM((BM, bn), jnp.bfloat16),
             pltpu.VMEM((BM, bn), jnp.bfloat16),
-            pltpu.SemaphoreType.DMA((len(txts),)),
-            pltpu.SemaphoreType.DMA((len(txts),)),
-            pltpu.SemaphoreType.DMA((Q // bn + len(txts),)),
+            pltpu.SemaphoreType.DMA((Q // bn,)),
+            pltpu.SemaphoreType.DMA((Q // bn,)),
+            pltpu.SemaphoreType.DMA((Q // bn + len(cuts),)),
             pltpu.SemaphoreType.DMA((4,)),
             pltpu.SemaphoreType.DMA((4,)),
             pltpu.SemaphoreType.DMA((4,)),
@@ -299,7 +324,7 @@
         compiler_params=pltpu.CompilerParams(vmem_limit_bytes=58 * 1024 * 1024),
         name="panel",
     )(*args)
-    return outs[0], list(outs[1 : 1 + len(txts)]), list(outs[1 + len(txts) :])
+    return outs[0], list(outs[1 : 1 + len(cuts)]), list(outs[1 + len(cuts) :])
 
 
 def combine_body(starts, factor, base, *refs):
@@ -315,18 +340,14 @@
     out[...] *= factor[0]
 
 
-def combine_call(factor, base, groups):
+def combine_call(factor, base, items):
     rows, D = base.shape
     br = 256
-    starts, specs, args = [], [], []
-    for group in groups:
-        lo = 0
-        for piece in group:
-            n = piece.shape[0] // br
-            starts.append((lo, lo + n))
-            specs.append(pl.BlockSpec((br, D), functools.partial(lambda lo, n, g: (jnp.clip(g - lo, 0, n - 1), 0), lo, n)))
-            args.append(piece)
-            lo += n
+    starts, specs = [], []
+    for lo, piece in items:
+        lo, n = lo // br, piece.shape[0] // br
+        starts.append((lo, lo + n))
+        specs.append(pl.BlockSpec((br, D), functools.partial(lambda lo, n, g: (jnp.clip(g - lo, 0, n - 1), 0), lo, n)))
     row = pl.BlockSpec((br, D), lambda g: (g, 0))
     return pl.pallas_call(
         functools.partial(combine_body, tuple(starts)),
@@ -337,29 +358,41 @@
         compiler_params=pltpu.CompilerParams(vmem_limit_bytes=32 * 1024 * 1024),
         cost_estimate=pl.CostEstimate(flops=rows * D * 64, bytes_accessed=16 * rows * D, transcendentals=0),
         name="combine",
-    )(factor.reshape(1), base, *args)
-
-
-def add_tail_body(factor, base, piece, out):
-    out[...] = base[...] + piece[...] * factor[0]
-
-
-def add_tail(factor, base, piece):
-    rows, D = base.shape
-    br = 256
-    n = piece.shape[0] // br
-    lo = rows // br - n
-    late = pl.BlockSpec((br, D), lambda g: (lo + g, 0))
+    )(factor.reshape(1), base, *[piece for _, piece in items])
+
+
+def add_rows_body(starts, factor, base, *refs):
+    refs = list(refs)
+    out = refs.pop()
+    g = pl.program_id(0)
+    for ref, (lo, hi) in zip(refs, starts):
+        @pl.when((g >= lo) & (g < hi))
+        def _():
+            out[...] = base[...] + ref[...] * factor[0]
+
+
+def add_rows(factor, base, row, pieces):
+    D = base.shape[1]
+    br = 128
+    first = row // br
+    starts, specs, lo = [], [], 0
+    for piece in pieces:
+        n = piece.shape[0] // br
+        starts.append((lo, lo + n))
+        specs.append(pl.BlockSpec((br, D), functools.partial(lambda lo, n, g: (jnp.clip(g - lo, 0, n - 1), 0), lo, n)))
+        lo += n
+    late = pl.BlockSpec((br, D), lambda g: (first + g, 0))
     return pl.pallas_call(
-        add_tail_body,
-        grid=(n,),
+        functools.partial(add_rows_body, tuple(starts)),
+        grid=(lo,),
         out_shape=jax.ShapeDtypeStruct(base.shape, jnp.float32),
-        in_specs=[pl.BlockSpec(memory_space=pltpu.SMEM), late, pl.BlockSpec((br, D), lambda g: (g, 0))],
+        in_specs=[pl.BlockSpec(memory_space=pltpu.SMEM), late, *specs],
         out_specs=late,
         input_output_aliases={1: 0},
         compiler_params=pltpu.CompilerParams(vmem_limit_bytes=32 * 1024 * 1024),
-        name="add_tail",
-    )(factor.reshape(1), base, piece)
+        cost_estimate=pl.CostEstimate(flops=lo * br * D * 64, bytes_accessed=12 * lo * br * D, transcendentals=0),
+        name="add_rows",
+    )(factor.reshape(1), base, *pieces)
 
 
 def solution(mesh):
@@ -378,13 +411,11 @@
         sc = jnp.stack([scale * LOG2E, logit_bias[0] * LOG2E])
         sums = jnp.zeros((4, 8, LANES), jnp.float32)
         ha, hb = slice(0, rows // 2), slice(rows // 2, rows)
-        x_cut = rows * 2 // 3
+        third = rows // 3
 
         img_c = swap(img, CORE)
-        x0 = swap(img[:x_cut], X)
-        x1 = swap(img[x_cut:], X)
-        xc0 = swap(x0, CORE)
-        xc1 = swap(x1, CORE)
+        x0, x1, x2 = (swap(img[k * third : (k + 1) * third], X) for k in range(3))
+        xc0, xc1, xc2 = (swap(a, CORE) for a in (x0, x1, x2))
         ya = swap(txt[ha], Y)
         zb = swap(txt[hb], Z)
         yza = swap(ya, Z)
@@ -392,33 +423,40 @@
         yb = swap(txt[hb], Y)
         za = swap(txt[ha], Z)
 
-        OC, X0, X1 = [img, img_c], [x0, xc0], [x1, xc1]
+        OC, X0, X1, X2 = [img, img_c], [x0, xc0], [x1, xc1], [x2, xc2]
         N2 = [None, None]
 
+        def reduce_x(acc, acc_c):
+            return swap(acc + swap(acc_c, CORE), X)
+
         sums, own, oc = panel(sc, sums, OC, N2, [txt], [None], diag=True)
-        sums, own, ax0 = panel(sc, sums, X0, N2, [txt], own)
-        sums, p_yz, accs = panel(sc, sums, OC + X0 + X1, oc + ax0 + N2, [yza, yzb], N2)
+        sums, own, ax = panel(sc, sums, X0 + X1, N2 + N2, [txt], own)
+        sums, p_yz, accs = panel(sc, sums, OC + X0 + X1 + X2, oc + ax + N2, [yza, yzb], N2)
         ry, rz = swap(p_yz[0], Z), swap(p_yz[1], Y)
-        sums, p_zayb, accs = panel(sc, sums, OC + X0 + X1, accs, [za, yb], N2)
-        oc, ax0, ax1 = accs[0:2], accs[2:4], accs[4:6]
+        sums, p_zayb, accs = panel(sc, sums, OC + X0 + X1 + X2, accs, [za, yb], N2)
+        ao, ac, a0, ac0, a1, ac1, a2, ac2 = accs
         fz, fy = swap(p_zayb[0], Z), swap(p_zayb[1], Y)
-        sums, p_yazb, ax0 = panel(sc, sums, X0, ax0, [ya, zb], [ry, rz])
-        gx0 = swap(ax0[0] + swap(ax0[1], CORE), X)
-        sums, p_yazb, accs = panel(sc, sums, OC + X1, oc + ax1, [ya, zb], p_yazb)
-        oc, ax1 = accs[0:2], accs[2:4]
-        gy, gz = swap(p_yazb[0], Y), swap(p_yazb[1], Z)
-        gc = swap(oc[1], CORE)
-        sums, own, ax1 = panel(sc, sums, X1, ax1, [txt], own)
-        gx1 = swap(ax1[0] + swap(ax1[1], CORE), X)
+        sums, p_yazb, (a0, ac0, ac1) = panel(sc, sums, [x0, xc0, xc1], [a0, ac0, ac1], [ya, zb], [ry, rz])
+        gx0 = reduce_x(a0, ac0)
+        sums, p_yazb, (a1, ac2) = panel(sc, sums, [x1, xc2], [a1, ac2], [ya, zb], p_yazb)
+        gx1 = reduce_x(a1, ac1)
+        sums, p_yazb, (ao, ac, a2) = panel(sc, sums, OC + [x2], [ao, ac, a2], [ya, zb], p_yazb, cuts=(512, 256, 256, 512))
+        gy0, gy1 = swap(p_yazb[0], Y), swap(p_yazb[1], Y)
+        gz0, gz1 = swap(p_yazb[3], Z), swap(p_yazb[2], Z)
+        gc = swap(ac, CORE)
+        sums, own, (a2, ac2) = panel(sc, sums, X2, [a2, ac2], [txt], own)
+        gx2 = reduce_x(a2, ac2)
 
         factor = scale / n_total
-        txt_pre = combine_call(jnp.ones((), jnp.float32), own[0], [[fz, fy]])
-        img_pre = combine_call(factor, oc[0], [[gc], [gx0]])
-        txt_grad = combine_call(factor, txt_pre, [[gy, gz]])
-        img_grad = add_tail(factor, img_pre, gx1)
+        txt_pre = combine_call(jnp.ones((), jnp.float32), own[0], [(0, fz), (rows // 2, fy)])
+        img_pre = combine_call(factor, ao, [(0, gc), (0, gx0), (third, gx1)])
+        txt_most = combine_call(factor, txt_pre, [(0, gy0), (2 * third, gz0)])
+        txt_grad = add_rows(factor, txt_most, third, [gy1, gz1])
+        img_grad = add_rows(factor, img_pre, 2 * third, [gx2])
         tot = jnp.sum(sums, axis=(1, 2))
-        for mask in (CORE, Y, Z, X):
-            tot = tot + swap(tot, mask)
+        tot = tot + swap(tot, CORE)
+        tot = tot + swap(tot, X)
+        tot = (tot + swap(tot, Y)) + (swap(tot, Z) + swap(tot, Y | Z))
         loss = -(tot[0:1] * LN2 + tot[1:2]) / n_total
         return loss, img_grad, txt_grad, tot[3:4] * factor, tot[2:3] / n_total
 

time: 926 us -> 940 us (1.015)
  Pallas kernels: 479 us -> 497 us
    pallas_call x7 -> x8, Pallas kernels: 452 us -> 461 us  [panel_call(): pl.pallas_call(functools.partial(panel_body, cfg), out_shape=out_shape, i...]
    ppermute x26 -> x33, starting transfers between devices: 26 us -> 32.1 us  [swap(): return lax.ppermute(a, axis, [(i, i ^ mask) for i in range(n_dev)])]
    ppermute x26 -> x33, waiting for transfers between devices: 381 us -> 382 us  [swap(): return lax.ppermute(a, axis, [(i, i ^ mask) for i in range(n_dev)])]
  transfers between devices with their start and end apart: 26 -> 33, of which waited for: 8 -> 14; matrix products, arithmetic and copies ran while one was open for 2% -> 1% of each run, Pallas kernels for 52% -> 53%
where the time goes in v2:
time: 940 us; the launch traced here: 935 us
  Pallas kernels  497 us (53%)
  waiting for transfers between devices  382 us (41%)
  starting transfers between devices  32.1 us (3%)
  local copies, waits for them, and re-layouts  9.46 us (1%)
    pallas_call x8, Pallas kernels, panel_call(): pl.pallas_call(functools.partial(panel_body, cfg), out_shape=out_shape, i...  461 us
    ppermute x33, waiting for transfers between devices, swap(): return lax.ppermute(a, axis, [(i, i ^ mask) for i in range(n_dev)])  382 us
    ppermute x33, starting transfers between devices, swap(): return lax.ppermute(a, axis, [(i, i ^ mask) for i in range(n_dev)])  32.1 us
    pallas_call x3, Pallas kernels, combine_call(): pl.pallas_call(functools.partial(combine_body, tuple(starts)), grid=(rows...  25.6 us
  transfers between devices with their start and end apart: 33, of which 14 were waited for; matrix products, arithmetic and copies ran while one was open for 1% of the time, Pallas kernels for 53%

profile of v2, /device:TPU:0, one launch (start us, length us, event | category | flops | bytes accessed | tf_op | source)
XLA Modules:
  0.0 935.5 jit_solution(13928885683948632780)
XLA Ops:
  1.4 4.2 fusion.1
  13.8 29.5 %collective-permute-done.3.refs_4_.refs_6_.refs_2_ = bf16[512,1536]{1,0:T(8,128)(2,1)} collective-permute-done((bf16[512,1536]{1,0:T(8,128)(2,1)S(1)}, bf16[512,1536]{1,0:T(8,128)(2,1)}, u32[]{:S(2)}, u32[]{:S(2)}) %collective-permute-start.3) | collective-permute-done | bytes 1572896 | tf_op jit(solution)/shard_map/ppermute | solution.py:403
  45.3 31.7 %collective-permute-done.1.refs_2_.refs_4_ = bf16[512,1536]{1,0:T(8,128)(2,1)} collective-permute-done((bf16[512,1536]{1,0:T(8,128)(2,1)S(1)}, bf16[512,1536]{1,0:T(8,128)(2,1)}, u32[]{:S(2)}, u32[]{:S(2)}) %collective-permute-start.1) | collective-permute-done | bytes 1572896 | tf_op jit(solution)/shard_map/ppermute | solution.py:403
  78.1 57.2 %panel.8 = (f32[4,8,256]{2,1,0:T(8,128)}, f32[1536,1536]{1,0:T(8,128)}, f32[1536,1536]{1,0:T(8,128)}, f32[1536,1536]{1,0:T(8,128)}) custom-call(f32[2]{0:T(128)} %pad_maximum_fusion.refs_0_, f32[4,8,256]{2,1,0:T(8,128)} %broadcast_in_dim.3.refs_1_, bf16[1536,1536]{1,0:T(8,128)(2,1)} %refs_2_.7, bf16[1536,1536]{1,0:T(8,128)(2,1)} %collective-permute-done.refs_3_, ...), custom_call_target="tpu_custom_call" | custom-call | flops 43486543872 | bytes 47185920 | tf_op jit(solution)/shard_map/panel/pallas_call | solution.py:302
  139.6 42.4 %panel.9 = (f32[4,8,256]{2,1,0:T(8,128)}, f32[1536,1536]{1,0:T(8,128)}, f32[512,1536]{1,0:T(8,128)}, f32[512,1536]{1,0:T(8,128)}, f32[512,1536]{1,0:T(8,128)}, /*index=5*/f32[512,1536]{1,0:T(8,128)}) custom-call(f32[2]{0:T(128)} %pad_maximum_fusion.refs_0_, f32[4,8,256]{2,1,0:T(8,128)} %get-tuple-element.60.refs_1_, ...), custom_call_target="tpu_custom_call" | custom-call | flops 28991029248 | bytes 31457280 | tf_op jit(solution)/shard_map/panel/pallas_call | solution.py:302
  182.0 57.5 %collective-permute-done.10.refs_11_ = bf16[768,1536]{1,0:T(8,128)(2,1)} collective-permute-done((bf16[768,1536]{1,0:T(8,128)(2,1)}, bf16[768,1536]{1,0:T(8,128)(2,1)}, u32[]{:S(2)}, u32[]{:S(2)}) %collective-permute-start.10) | collective-permute-done | bytes 2359328 | tf_op jit(solution)/shard_map/ppermute | solution.py:403
  241.0 105.3 %panel.10 = (f32[4,8,256]{2,1,0:T(8,128)}, f32[768,1536]{1,0:T(8,128)}, f32[768,1536]{1,0:T(8,128)}, f32[1536,1536]{1,0:T(8,128)}, f32[1536,1536]{1,0:T(8,128)},...) custom-call(f32[2]{0:T(128)} %pad_maximum_fusion.refs_0_, ...), custom_call_target="tpu_custom_call", output_to_operand_aliasing={{3}: (12, {}), {4}: (13, {}), {5}: (14, {}), {6}: (15, {}),... | custom-call | flops 86973087744 | bytes 94371840 | tf_op jit(solution)/shard_map/panel/pallas_call | solution.py:302
  348.4 103.8 %panel.11 = (f32[4,8,256]{2,1,0:T(8,128)}, f32[768,1536]{1,0:T(8,128)}, f32[768,1536]{1,0:T(8,128)}, f32[1536,1536]{1,0:T(8,128)}, f32[1536,1536]{1,0:T(8,128)},...) custom-call(f32[2]{0:T(128)} %pad_maximum_fusion.refs_0_, ...), custom_call_target="tpu_custom_call", output_to_operand_aliasing={{3}: (12, {}), {4}: (13, {}), {5}: (14, {}), {6}: (15, {}),... | custom-call | flops 86973087744 | bytes 94371840 | tf_op jit(solution)/shard_map/panel/pallas_call | solution.py:302
  454.2 33.6 %panel.12 = (f32[4,8,256]{2,1,0:T(8,128)}, f32[768,1536]{1,0:T(8,128)}, f32[768,1536]{1,0:T(8,128)}, f32[512,1536]{1,0:T(8,128)}, f32[512,1536]{1,0:T(8,128)}, /*index=5*/f32[512,1536]{1,0:T(8,128)}) custom-call(f32[2]{0:T(128)} %pad_maximum_fusion.refs_0_, ...), custom_call_target="tpu_custom_call", output_to_operand_aliasing={{3}: (9, {}), {4}: (10, {}), {5}: (11, {})} | custom-call | flops 21743271936 | bytes 23592960 | tf_op jit(solution)/shard_map/panel/pallas_call | solution.py:302
  487.9 26.5 %panel.13 = (f32[4,8,256]{2,1,0:T(8,128)}, f32[768,1536]{1,0:T(8,128)}, f32[768,1536]{1,0:T(8,128)}, f32[512,1536]{1,0:T(8,128)}, f32[512,1536]{1,0:T(8,128)}) custom-call(f32[2]{0:T(128)} %pad_maximum_fusion.refs_0_, f32[4,8,256]{2,1,0:T(8,128)} %get-tuple-element.84.refs_1_, ...), custom_call_target="tpu_custom_call", output_to_operand_aliasing={{3}: (8, {}), {4}: (9, {})} | custom-call | flops 14495514624 | bytes 15728640 | tf_op jit(solution)/shard_map/panel/pallas_call | solution.py:302
  514.3 66.2 %panel.14 = (f32[4,8,256]{2,1,0:T(8,128)}, f32[512,1536]{1,0:T(8,128)}, f32[256,1536]{1,0:T(8,128)}, f32[256,1536]{1,0:T(8,128)}, f32[512,1536]{1,0:T(8,128)}, /...) custom-call(f32[2]{0:T(128)} %pad_maximum_fusion.refs_0_, ...), custom_call_target="tpu_custom_call", output_to_operand_aliasing={{5}: (9, {}), {6}: (10, {}), {7}: (11, {})} | custom-call | flops 50734301184 | bytes 55050240 | tf_op jit(solution)/shard_map/panel/pallas_call | solution.py:302
  581.1 26.3 %panel.15 = (f32[4,8,256]{2,1,0:T(8,128)}, f32[1536,1536]{1,0:T(8,128)}, f32[512,1536]{1,0:T(8,128)}, f32[512,1536]{1,0:T(8,128)}) custom-call(f32[2]{0:T(128)} %pad_maximum_fusion.refs_0_, f32[4,8,256]{2,1,0:T(8,128)} %get-tuple-element.95.refs_1_, ...), custom_call_target="tpu_custom_call", output_to_operand_aliasing={{2}: (6, {}), {3}: (7, {})} | custom-call | flops 14495514624 | bytes 15728640 | tf_op jit(solution)/shard_map/panel/pallas_call | solution.py:302
  614.8 2.9 collective-permute-done.19
  621.7 3.2 collective-permute-done.17
  632.0 93.9 %collective-permute-done.31.refs_0_ = f32[256,1536]{1,0:T(8,128)S(1)} collective-permute-done((f32[256,1536]{1,0:T(8,128)}, f32[256,1536]{1,0:T(8,128)S(1)}, u32[]{:S(2)}, u32[]{:S(2)}) %collective-permute-start.31) | collective-permute-done | bytes 1572896 | tf_op jit(solution)/shard_map/ppermute | solution.py:403
  736.7 9.9 %combine.4.base = f32[1536,1536]{1,0:T(8,128)S(1)} custom-call(f32[1]{0:T(128)} %constant.17.clone.1.factor, f32[1536,1536]{1,0:T(8,128)} %get-tuple-element.108.base, f32[768,1536]{1,0:T(8,128)} %collective-permute-done.27.refs_0_, f32[768,1536]{1,0:T(8,128)} %collective-permute-done.28.refs_1_), custom_call_target="tpu_custom_call" | custom-call | flops 150994944 | bytes 37748736 | tf_op jit(solution)/shard_map/combine/pallas_call | solution.py:352
  749.9 5.1 combine.5.base
  754.9 12.1 %collective-permute-done.32.refs_1_ = f32[256,1536]{1,0:T(8,128)} collective-permute-done((f32[256,1536]{1,0:T(8,128)}, f32[256,1536]{1,0:T(8,128)}, u32[]{:S(2)}, u32[]{:S(2)}) %collective-permute-start.32) | collective-permute-done | bytes 1572896 | tf_op jit(solution)/shard_map/ppermute | solution.py:403
  767.0 4.8 add_rows.3
  771.8 25.1 %collective-permute-done.22.refs_1_ = f32[512,1536]{1,0:T(8,128)} collective-permute-done((f32[512,1536]{1,0:T(8,128)S(1)}, f32[512,1536]{1,0:T(8,128)}, u32[]{:S(2)}, u32[]{:S(2)}) %collective-permute-start.22) | collective-permute-done | bytes 3145760 | tf_op jit(solution)/shard_map/ppermute | solution.py:403
  796.9 67.4 %collective-permute-done.24.refs_2_ = f32[512,1536]{1,0:T(8,128)} collective-permute-done((f32[512,1536]{1,0:T(8,128)S(1)}, f32[512,1536]{1,0:T(8,128)}, u32[]{:S(2)}, u32[]{:S(2)}) %collective-permute-start.24) | collective-permute-done | bytes 3145760 | tf_op jit(solution)/shard_map/ppermute | solution.py:403
  864.4 10.6 %combine.3.base = f32[1536,1536]{1,0:T(8,128)} custom-call(f32[1]{0:T(128)S(6)} %div.10.factor, f32[1536,1536]{1,0:T(8,128)S(1)} %bitcast.1, f32[1536,1536]{1,0:T(8,128)} %collective-permute-done.20.refs_0_, f32[512,1536]{1,0:T(8,128)} %collective-permute-done.22.refs_1_, f32[512,1536]{1,0:T(8,128)} %collective-permute-done.24.refs_2_), custom_call_target="tpu_custom_call" | custom-call | flops 150994944 | bytes 37748736 | tf_op jit(solution)/shard_map/combine/pallas_call | solution.py:352
  875.0 52.0 %collective-permute-done.26.refs_0_ = f32[512,1536]{1,0:T(8,128)} collective-permute-done((f32[512,1536]{1,0:T(8,128)}, f32[512,1536]{1,0:T(8,128)}, u32[]{:S(2)}, u32[]{:S(2)}) %collective-permute-start.26) | collective-permute-done | bytes 3145760 | tf_op jit(solution)/shard_map/ppermute | solution.py:403
  927.0 4.9 add_rows.2
  (88 shorter events, 50.9 us)
Async XLA Ops:
  0.6 76.5 %collective-permute-start = (bf16[1536,1536]{1,0:T(8,128)(2,1)}, bf16[1536,1536]{1,0:T(8,128)(2,1)}, u32[]{:S(2)}, u32[]{:S(2)}) collective-permute-start(bf16[1536,1536]{1,0:T(8,128)(2,1)} %refs_2_.7), channel_id=1, source_target_pairs={{0,1},{1,0},{2,3},{3,2},{4,5},{5,4},{6,7},{7,6},{8,9},{9,8},{10,11... | collective-permute-start | bytes 14155784 | tf_op jit(solution)/shard_map/ppermute | solution.py:403
  7.9 69.1 %collective-permute-start.1 = (bf16[512,1536]{1,0:T(8,128)(2,1)S(1)}, bf16[512,1536]{1,0:T(8,128)(2,1)}, u32[]{:S(2)}, u32[]{:S(2)}) collective-permute-start(bf16[512,1536]{1,0:T(8,128)(2,1)S(1)} %get-tuple-element.119), channel_id=1, source_target_pairs={{0,2},{1,3},{2,0},{3,1},{4,6},{5,7},{6,4},{7,5},{8,10},{9,11},{10,... | collective-permute-start | bytes 4718600 | tf_op jit(solution)/shard_map/ppermute | solution.py:403
  7.9 127.4 %collective-permute-start.5 = (bf16[512,1536]{1,0:T(8,128)(2,1)}, bf16[512,1536]{1,0:T(8,128)(2,1)}, u32[]{:S(2)}, u32[]{:S(2)}) collective-permute-start(bf16[512,1536]{1,0:T(8,128)(2,1)} %get-tuple-element.117), channel_id=1, source_target_pairs={{0,2},{1,3},{2,0},{3,1},{4,6},{5,7},{6,4},{7,5},{8,10},{9,11},{10,... | collective-permute-start | bytes 4718600 | tf_op jit(solution)/shard_map/ppermute | solution.py:403
  10.3 127.2 %collective-permute-start.9 = (bf16[768,1536]{1,0:T(8,128)(2,1)S(1)}, bf16[768,1536]{1,0:T(8,128)(2,1)}, u32[]{:S(2)}, u32[]{:S(2)}) collective-permute-start(bf16[768,1536]{1,0:T(8,128)(2,1)S(1)} %get-tuple-element.115), channel_id=1, source_target_pairs={{0,8},{1,9},{2,10},{3,11},{4,12},{5,13},{6,14},{7,15},{8,0},{9,1},... | collective-permute-start | bytes 7077896 | tf_op jit(solution)/shard_map/ppermute | solution.py:403
  43.3 95.7 %collective-permute-start.7 = (bf16[768,1536]{1,0:T(8,128)(2,1)S(1)}, bf16[768,1536]{1,0:T(8,128)(2,1)}, u32[]{:S(2)}, u32[]{:S(2)}) collective-permute-start(bf16[768,1536]{1,0:T(8,128)(2,1)S(1)} %get-tuple-element.116), channel_id=1, source_target_pairs={{0,4},{1,5},{2,6},{3,7},{4,0},{5,1},{6,2},{7,3},{8,12},{9,13},{10,... | collective-permute-start | bytes 7077896 | tf_op jit(solution)/shard_map/ppermute | solution.py:403
  77.0 62.0 %collective-permute-start.4 = (bf16[512,1536]{1,0:T(8,128)(2,1)}, bf16[512,1536]{1,0:T(8,128)(2,1)}, u32[]{:S(2)}, u32[]{:S(2)}) collective-permute-start(bf16[512,1536]{1,0:T(8,128)(2,1)} %collective-permute-done.3.refs_4_.refs_6_.refs_2_), channel_id=1, source_target_pairs={{0,1},{1,0},{2,3},{3,2},{4,5},{5,4},{6,7},{7,6},{8,9},{9,8},{10,11... | collective-permute-start | bytes 4718600 | tf_op jit(solution)/shard_map/ppermute | solution.py:403
  77.1 62.5 %collective-permute-start.2 = (bf16[512,1536]{1,0:T(8,128)(2,1)}, bf16[512,1536]{1,0:T(8,128)(2,1)}, u32[]{:S(2)}, u32[]{:S(2)}) collective-permute-start(bf16[512,1536]{1,0:T(8,128)(2,1)} %collective-permute-done.1.refs_2_.refs_4_), channel_id=1, source_target_pairs={{0,1},{1,0},{2,3},{3,2},{4,5},{5,4},{6,7},{7,6},{8,9},{9,8},{10,11... | collective-permute-start | bytes 4718600 | tf_op jit(solution)/shard_map/ppermute | solution.py:403
  135.3 213.1 %collective-permute-start.12 = (bf16[768,1536]{1,0:T(8,128)(2,1)S(1)}, bf16[768,1536]{1,0:T(8,128)(2,1)}, u32[]{:S(2)}, u32[]{:S(2)}) collective-permute-start(bf16[768,1536]{1,0:T(8,128)(2,1)S(1)} %get-tuple-element.115), channel_id=1, source_target_pairs={{0,4},{1,5},{2,6},{3,7},{4,0},{5,1},{6,2},{7,3},{8,12},{9,13},{10,... | collective-permute-start | bytes 7077896 | tf_op jit(solution)/shard_map/ppermute | solution.py:403
  137.4 211.0 %collective-permute-start.11 = (bf16[768,1536]{1,0:T(8,128)(2,1)S(1)}, bf16[768,1536]{1,0:T(8,128)(2,1)}, u32[]{:S(2)}, u32[]{:S(2)}) collective-permute-start(bf16[768,1536]{1,0:T(8,128)(2,1)S(1)} %get-tuple-element.116), channel_id=1, source_target_pairs={{0,8},{1,9},{2,10},{3,11},{4,12},{5,13},{6,14},{7,15},{8,0},{9,1},... | collective-permute-start | bytes 7077896 | tf_op jit(solution)/shard_map/ppermute | solution.py:403
  139.0 100.5 %collective-permute-start.10 = (bf16[768,1536]{1,0:T(8,128)(2,1)}, bf16[768,1536]{1,0:T(8,128)(2,1)}, u32[]{:S(2)}, u32[]{:S(2)}) collective-permute-start(bf16[768,1536]{1,0:T(8,128)(2,1)} %collective-permute-done.9.refs_6_.refs_5_), channel_id=1, source_target_pairs={{0,4},{1,5},{2,6},{3,7},{4,0},{5,1},{6,2},{7,3},{8,12},{9,13},{10,... | collective-permute-start | bytes 7077896 | tf_op jit(solution)/shard_map/ppermute | solution.py:403
  139.6 101.4 %collective-permute-start.8 = (bf16[768,1536]{1,0:T(8,128)(2,1)}, bf16[768,1536]{1,0:T(8,128)(2,1)}, u32[]{:S(2)}, u32[]{:S(2)}) collective-permute-start(bf16[768,1536]{1,0:T(8,128)(2,1)} %collective-permute-done.7.refs_5_.refs_4_), channel_id=1, source_target_pairs={{0,8},{1,9},{2,10},{3,11},{4,12},{5,13},{6,14},{7,15},{8,0},{9,1},... | collective-permute-start | bytes 7077896 | tf_op jit(solution)/shard_map/ppermute | solution.py:403
  346.3 107.9 %collective-permute-start.13 = (f32[768,1536]{1,0:T(8,128)}, f32[768,1536]{1,0:T(8,128)}, u32[]{:S(2)}, u32[]{:S(2)}) collective-permute-start(f32[768,1536]{1,0:T(8,128)} %get-tuple-element.79), channel_id=1, source_target_pairs={{0,8},{1,9},{2,10},{3,11},{4,12},{5,13},{6,14},{7,15},{8,0},{9,1},... | collective-permute-start | bytes 14155784 | tf_op jit(solution)/shard_map/ppermute | solution.py:403
  347.9 106.3 %collective-permute-start.14 = (f32[768,1536]{1,0:T(8,128)}, f32[768,1536]{1,0:T(8,128)}, u32[]{:S(2)}, u32[]{:S(2)}) collective-permute-start(f32[768,1536]{1,0:T(8,128)} %get-tuple-element.80), channel_id=1, source_target_pairs={{0,4},{1,5},{2,6},{3,7},{4,0},{5,1},{6,2},{7,3},{8,12},{9,13},{10,... | collective-permute-start | bytes 14155784 | tf_op jit(solution)/shard_map/ppermute | solution.py:403
  452.2 157.4 %collective-permute-start.27 = (f32[768,1536]{1,0:T(8,128)}, f32[768,1536]{1,0:T(8,128)}, u32[]{:S(2)}, u32[]{:S(2)}) collective-permute-start(f32[768,1536]{1,0:T(8,128)} %get-tuple-element.109), channel_id=1, source_target_pairs={{0,8},{1,9},{2,10},{3,11},{4,12},{5,13},{6,14},{7,15},{8,0},{9,1},... | collective-permute-start | bytes 14155784 | tf_op jit(solution)/shard_map/ppermute | solution.py:403
  452.6 160.7 %collective-permute-start.28 = (f32[768,1536]{1,0:T(8,128)}, f32[768,1536]{1,0:T(8,128)}, u32[]{:S(2)}, u32[]{:S(2)}) collective-permute-start(f32[768,1536]{1,0:T(8,128)} %get-tuple-element.110), channel_id=1, source_target_pairs={{0,4},{1,5},{2,6},{3,7},{4,0},{5,1},{6,2},{7,3},{8,12},{9,13},{10,... | collective-permute-start | bytes 14155784 | tf_op jit(solution)/shard_map/ppermute | solution.py:403
  580.6 283.8 %collective-permute-start.20 = (f32[1536,1536]{1,0:T(8,128)}, f32[1536,1536]{1,0:T(8,128)}, u32[]{:S(2)}, u32[]{:S(2)}) collective-permute-start(f32[1536,1536]{1,0:T(8,128)} %get-tuple-element.101), channel_id=1, source_target_pairs={{0,1},{1,0},{2,3},{3,2},{4,5},{5,4},{6,7},{7,6},{8,9},{9,8},{10,11... | collective-permute-start | bytes 28311560 | tf_op jit(solution)/shard_map/ppermute | solution.py:403
  580.6 44.6 %collective-permute-start.21 = (f32[512,1536]{1,0:T(8,128)}, f32[512,1536]{1,0:T(8,128)S(1)}, u32[]{:S(2)}, u32[]{:S(2)}) collective-permute-start(f32[512,1536]{1,0:T(8,128)} %get-tuple-element.103), channel_id=1, source_target_pairs={{0,1},{1,0},{2,3},{3,2},{4,5},{5,4},{6,7},{7,6},{8,9},{9,8},{10,11... | collective-permute-start | bytes 9437192 | tf_op jit(solution)/shard_map/ppermute | solution.py:403
  613.3 114.1 %collective-permute-start.25 = (f32[512,1536]{1,0:T(8,128)}, f32[512,1536]{1,0:T(8,128)S(1)}, u32[]{:S(2)}, u32[]{:S(2)}) collective-permute-start(f32[512,1536]{1,0:T(8,128)} %get-tuple-element.107), channel_id=1, source_target_pairs={{0,1},{1,0},{2,3},{3,2},{4,5},{5,4},{6,7},{7,6},{8,9},{9,8},{10,11... | collective-permute-start | bytes 9437192 | tf_op jit(solution)/shard_map/ppermute | solution.py:403
  624.9 105.2 %collective-permute-start.29 = (f32[512,1536]{1,0:T(8,128)}, f32[512,1536]{1,0:T(8,128)S(1)}, u32[]{:S(2)}, u32[]{:S(2)}) collective-permute-start(f32[512,1536]{1,0:T(8,128)} %get-tuple-element.111), channel_id=1, source_target_pairs={{0,4},{1,5},{2,6},{3,7},{4,0},{5,1},{6,2},{7,3},{8,12},{9,13},{10,... | collective-permute-start | bytes 9437192 | tf_op jit(solution)/shard_map/ppermute | solution.py:403
  625.3 108.1 %collective-permute-start.30 = (f32[512,1536]{1,0:T(8,128)}, f32[512,1536]{1,0:T(8,128)S(1)}, u32[]{:S(2)}, u32[]{:S(2)}) collective-permute-start(f32[512,1536]{1,0:T(8,128)} %get-tuple-element.112), channel_id=1, source_target_pairs={{0,8},{1,9},{2,10},{3,11},{4,12},{5,13},{6,14},{7,15},{8,0},{9,1},... | collective-permute-start | bytes 9437192 | tf_op jit(solution)/shard_map/ppermute | solution.py:403
  627.0 98.8 %collective-permute-start.31 = (f32[256,1536]{1,0:T(8,128)}, f32[256,1536]{1,0:T(8,128)S(1)}, u32[]{:S(2)}, u32[]{:S(2)}) collective-permute-start(f32[256,1536]{1,0:T(8,128)} %get-tuple-element.113), channel_id=1, source_target_pairs={{0,4},{1,5},{2,6},{3,7},{4,0},{5,1},{6,2},{7,3},{8,12},{9,13},{10,... | collective-permute-start | bytes 4718600 | tf_op jit(solution)/shard_map/ppermute | solution.py:403
  725.9 71.1 %collective-permute-start.22 = (f32[512,1536]{1,0:T(8,128)S(1)}, f32[512,1536]{1,0:T(8,128)}, u32[]{:S(2)}, u32[]{:S(2)}) collective-permute-start(f32[512,1536]{1,0:T(8,128)S(1)} %add.33), channel_id=1, source_target_pairs={{0,2},{1,3},{2,0},{3,1},{4,6},{5,7},{6,4},{7,5},{8,10},{9,11},{10,... | collective-permute-start | bytes 9437192 | tf_op jit(solution)/shard_map/ppermute | solution.py:403
  727.4 137.0 %collective-permute-start.24 = (f32[512,1536]{1,0:T(8,128)S(1)}, f32[512,1536]{1,0:T(8,128)}, u32[]{:S(2)}, u32[]{:S(2)}) collective-permute-start(f32[512,1536]{1,0:T(8,128)S(1)} %add.34), channel_id=1, source_target_pairs={{0,2},{1,3},{2,0},{3,1},{4,6},{5,7},{6,4},{7,5},{8,10},{9,11},{10,... | collective-permute-start | bytes 9437192 | tf_op jit(solution)/shard_map/ppermute | solution.py:403
  731.9 195.1 %collective-permute-start.26 = (f32[512,1536]{1,0:T(8,128)}, f32[512,1536]{1,0:T(8,128)}, u32[]{:S(2)}, u32[]{:S(2)}) collective-permute-start(f32[512,1536]{1,0:T(8,128)} %add.35), channel_id=1, source_target_pairs={{0,2},{1,3},{2,0},{3,1},{4,6},{5,7},{6,4},{7,5},{8,10},{9,11},{10,... | collective-permute-start | bytes 9437192 | tf_op jit(solution)/shard_map/ppermute | solution.py:403
  (19 other events, 623.3 us)

commit v3 on v2

--- a/solution.py
+++ b/solution.py
@@ -24,6 +24,7 @@
     imgs, txts = take(nseg), take(npc)
     tins = take(sum(tin_flags))
     iins = take(sum(seg_acc))
+    zero = None if all(seg_acc) else take(1)[0]
     (sums,) = take(1)
     tos, ios = take(len(cuts)), take(nseg)
     T, TO, I, A, S, C, CR, tsem, osem, fsem, isem, asem, wsem = refs
@@ -89,8 +90,8 @@
         def one(k):
             rows = pl.ds((g - starts[k]) * BM, BM)
             pltpu.make_async_copy(imgs[k].at[rows], I.at[g % 4], isem.at[g % 4]).start()
-            if seg_acc[k]:
-                pltpu.make_async_copy(acc_src[k].at[rows], A.at[g % 4], asem.at[g % 4]).start()
+            src = acc_src[k].at[rows] if seg_acc[k] else zero
+            pltpu.make_async_copy(src, A.at[g % 4], asem.at[g % 4]).start()
 
         when_seg(g, one)
 
@@ -98,13 +99,7 @@
         pltpu.make_async_copy(imgs[0].at[pl.ds(0, BM)], I.at[g % 4], isem.at[g % 4]).wait()
 
     def open_acc(g):
-        def one(k):
-            if seg_acc[k]:
-                pltpu.make_async_copy(acc_src[k].at[pl.ds(0, BM)], A.at[g % 4], asem.at[g % 4]).wait()
-            else:
-                A[g % 4] = jnp.zeros((BM, D), jnp.float32)
-
-        when_seg(g, one)
+        pltpu.make_async_copy(ios[0].at[pl.ds(0, BM)], A.at[g % 4], asem.at[g % 4]).wait()
 
     def put(g):
         def one(k):
@@ -289,6 +284,8 @@
     na = len(args)
     ia = [a for a in iins if a is not None]
     args += ia
+    if len(ia) < len(iins):
+        args.append(jnp.zeros((BM, D), jnp.float32))
     out_shape = [jax.ShapeDtypeStruct(sums.shape, jnp.float32)]
     out_shape += [jax.ShapeDtypeStruct((c, D), jnp.float32) for c in cuts] + [jax.ShapeDtypeStruct(a.shape, jnp.float32) for a in imgs]
     alias = {}

time: 940 us -> 937 us (level)
  transfers between devices with their start and end apart: 33 -> 33, of which waited for: 14 -> 14; matrix products, arithmetic and copies ran while one was open for 1% -> 2% of each run, Pallas kernels for 53% -> 52%
where the time goes in v3:
time: 937 us; the launch traced here: 933 us
  Pallas kernels  491 us (52%)
  waiting for transfers between devices  383 us (41%)
  starting transfers between devices  32.1 us (3%)
  local copies, waits for them, and re-layouts  11.4 us (1%)
    pallas_call x8, Pallas kernels, panel_call(): pl.pallas_call(functools.partial(panel_body, cfg), out_shape=out_shape, i...  456 us
    ppermute x33, waiting for transfers between devices, swap(): return lax.ppermute(a, axis, [(i, i ^ mask) for i in range(n_dev)])  383 us
    ppermute x33, starting transfers between devices, swap(): return lax.ppermute(a, axis, [(i, i ^ mask) for i in range(n_dev)])  32.1 us
    pallas_call x3, Pallas kernels, combine_call(): pl.pallas_call(functools.partial(combine_body, tuple(starts)), grid=(rows...  25.6 us
  transfers between devices with their start and end apart: 33, of which 14 were waited for; matrix products, arithmetic and copies ran while one was open for 2% of the time, Pallas kernels for 52%

profile of v3, /device:TPU:0, one launch (start us, length us, event | category | flops | bytes accessed | tf_op | source)
XLA Modules:
  0.0 932.8 jit_solution(17370907987913916590)
XLA Ops:
  1.4 4.2 fusion.1
  13.7 29.5 %collective-permute-done.3.refs_4_.refs_6_.refs_2_ = bf16[512,1536]{1,0:T(8,128)(2,1)} collective-permute-done((bf16[512,1536]{1,0:T(8,128)(2,1)S(1)}, bf16[512,1536]{1,0:T(8,128)(2,1)}, u32[]{:S(2)}, u32[]{:S(2)}) %collective-permute-start.3) | collective-permute-done | bytes 1572896 | tf_op jit(solution)/shard_map/ppermute | solution.py:400
  45.3 31.7 %collective-permute-done.1.refs_2_.refs_4_ = bf16[512,1536]{1,0:T(8,128)(2,1)} collective-permute-done((bf16[512,1536]{1,0:T(8,128)(2,1)S(1)}, bf16[512,1536]{1,0:T(8,128)(2,1)}, u32[]{:S(2)}, u32[]{:S(2)}) %collective-permute-start.1) | collective-permute-done | bytes 1572896 | tf_op jit(solution)/shard_map/ppermute | solution.py:400
  80.1 56.0 %panel.8 = (f32[4,8,256]{2,1,0:T(8,128)}, f32[1536,1536]{1,0:T(8,128)}, f32[1536,1536]{1,0:T(8,128)}, f32[1536,1536]{1,0:T(8,128)}) custom-call(f32[2]{0:T(128)} %pad_maximum_fusion.refs_0_, f32[4,8,256]{2,1,0:T(8,128)} %broadcast_in_dim.3.refs_1_, bf16[1536,1536]{1,0:T(8,128)(2,1)} %refs_2_.7, bf16[1536,1536]{1,0:T(8,128)(2,1)} %collective-permute-done.refs_3_, ...), custom_call_target="tpu_custom_call" | custom-call | flops 43486543872 | bytes 47185920 | tf_op jit(solution)/shard_map/panel/pallas_call | solution.py:299
  140.4 41.7 %panel.9 = (f32[4,8,256]{2,1,0:T(8,128)}, f32[1536,1536]{1,0:T(8,128)}, f32[512,1536]{1,0:T(8,128)}, f32[512,1536]{1,0:T(8,128)}, f32[512,1536]{1,0:T(8,128)}, /*index=5*/f32[512,1536]{1,0:T(8,128)}) custom-call(f32[2]{0:T(128)} %pad_maximum_fusion.refs_0_, f32[4,8,256]{2,1,0:T(8,128)} %get-tuple-element.60.refs_1_, ...), custom_call_target="tpu_custom_call" | custom-call | flops 28991029248 | bytes 31457280 | tf_op jit(solution)/shard_map/panel/pallas_call | solution.py:299
  182.1 58.2 %collective-permute-done.10.refs_11_ = bf16[768,1536]{1,0:T(8,128)(2,1)} collective-permute-done((bf16[768,1536]{1,0:T(8,128)(2,1)}, bf16[768,1536]{1,0:T(8,128)(2,1)}, u32[]{:S(2)}, u32[]{:S(2)}) %collective-permute-start.10) | collective-permute-done | bytes 2359328 | tf_op jit(solution)/shard_map/ppermute | solution.py:400
  241.7 103.2 %panel.10 = (f32[4,8,256]{2,1,0:T(8,128)}, f32[768,1536]{1,0:T(8,128)}, f32[768,1536]{1,0:T(8,128)}, f32[1536,1536]{1,0:T(8,128)}, f32[1536,1536]{1,0:T(8,128)},...) custom-call(f32[2]{0:T(128)} %pad_maximum_fusion.refs_0_, ...), custom_call_target="tpu_custom_call", output_to_operand_aliasing={{3}: (12, {}), {4}: (13, {}), {5}: (14, {}), {6}: (15, {}),... | custom-call | flops 86973087744 | bytes 94371840 | tf_op jit(solution)/shard_map/panel/pallas_call | solution.py:299
  347.0 103.2 %panel.11 = (f32[4,8,256]{2,1,0:T(8,128)}, f32[768,1536]{1,0:T(8,128)}, f32[768,1536]{1,0:T(8,128)}, f32[1536,1536]{1,0:T(8,128)}, f32[1536,1536]{1,0:T(8,128)},...) custom-call(f32[2]{0:T(128)} %pad_maximum_fusion.refs_0_, ...), custom_call_target="tpu_custom_call", output_to_operand_aliasing={{3}: (12, {}), {4}: (13, {}), {5}: (14, {}), {6}: (15, {}),... | custom-call | flops 86973087744 | bytes 94371840 | tf_op jit(solution)/shard_map/panel/pallas_call | solution.py:299
  452.2 33.4 %panel.12 = (f32[4,8,256]{2,1,0:T(8,128)}, f32[768,1536]{1,0:T(8,128)}, f32[768,1536]{1,0:T(8,128)}, f32[512,1536]{1,0:T(8,128)}, f32[512,1536]{1,0:T(8,128)}, /*index=5*/f32[512,1536]{1,0:T(8,128)}) custom-call(f32[2]{0:T(128)} %pad_maximum_fusion.refs_0_, ...), custom_call_target="tpu_custom_call", output_to_operand_aliasing={{3}: (9, {}), {4}: (10, {}), {5}: (11, {})} | custom-call | flops 21743271936 | bytes 23592960 | tf_op jit(solution)/shard_map/panel/pallas_call | solution.py:299
  485.6 26.4 %panel.13 = (f32[4,8,256]{2,1,0:T(8,128)}, f32[768,1536]{1,0:T(8,128)}, f32[768,1536]{1,0:T(8,128)}, f32[512,1536]{1,0:T(8,128)}, f32[512,1536]{1,0:T(8,128)}) custom-call(f32[2]{0:T(128)} %pad_maximum_fusion.refs_0_, f32[4,8,256]{2,1,0:T(8,128)} %get-tuple-element.84.refs_1_, ...), custom_call_target="tpu_custom_call", output_to_operand_aliasing={{3}: (8, {}), {4}: (9, {})} | custom-call | flops 14495514624 | bytes 15728640 | tf_op jit(solution)/shard_map/panel/pallas_call | solution.py:299
  512.1 65.9 %panel.14 = (f32[4,8,256]{2,1,0:T(8,128)}, f32[512,1536]{1,0:T(8,128)}, f32[256,1536]{1,0:T(8,128)}, f32[256,1536]{1,0:T(8,128)}, f32[512,1536]{1,0:T(8,128)}, /...) custom-call(f32[2]{0:T(128)} %pad_maximum_fusion.refs_0_, ...), custom_call_target="tpu_custom_call", output_to_operand_aliasing={{5}: (9, {}), {6}: (10, {}), {7}: (11, {})} | custom-call | flops 50734301184 | bytes 55050240 | tf_op jit(solution)/shard_map/panel/pallas_call | solution.py:299
  578.5 26.3 %panel.15 = (f32[4,8,256]{2,1,0:T(8,128)}, f32[1536,1536]{1,0:T(8,128)}, f32[512,1536]{1,0:T(8,128)}, f32[512,1536]{1,0:T(8,128)}) custom-call(f32[2]{0:T(128)} %pad_maximum_fusion.refs_0_, f32[4,8,256]{2,1,0:T(8,128)} %get-tuple-element.95.refs_1_, ...), custom_call_target="tpu_custom_call", output_to_operand_aliasing={{2}: (6, {}), {3}: (7, {})} | custom-call | flops 14495514624 | bytes 15728640 | tf_op jit(solution)/shard_map/panel/pallas_call | solution.py:299
  612.2 2.9 collective-permute-done.19
  619.0 3.2 collective-permute-done.17
  629.3 93.9 %collective-permute-done.31.refs_0_ = f32[256,1536]{1,0:T(8,128)S(1)} collective-permute-done((f32[256,1536]{1,0:T(8,128)}, f32[256,1536]{1,0:T(8,128)S(1)}, u32[]{:S(2)}, u32[]{:S(2)}) %collective-permute-start.31) | collective-permute-done | bytes 1572896 | tf_op jit(solution)/shard_map/ppermute | solution.py:400
  734.1 9.9 %combine.4.base = f32[1536,1536]{1,0:T(8,128)S(1)} custom-call(f32[1]{0:T(128)} %constant.18.clone.1.factor, f32[1536,1536]{1,0:T(8,128)} %get-tuple-element.108.base, f32[768,1536]{1,0:T(8,128)} %collective-permute-done.27.refs_0_, f32[768,1536]{1,0:T(8,128)} %collective-permute-done.28.refs_1_), custom_call_target="tpu_custom_call" | custom-call | flops 150994944 | bytes 37748736 | tf_op jit(solution)/shard_map/combine/pallas_call | solution.py:349
  747.2 5.1 combine.5.base
  752.3 12.1 %collective-permute-done.32.refs_1_ = f32[256,1536]{1,0:T(8,128)} collective-permute-done((f32[256,1536]{1,0:T(8,128)}, f32[256,1536]{1,0:T(8,128)}, u32[]{:S(2)}, u32[]{:S(2)}) %collective-permute-start.32) | collective-permute-done | bytes 1572896 | tf_op jit(solution)/shard_map/ppermute | solution.py:400
  764.4 4.8 add_rows.3
  769.2 25.1 %collective-permute-done.22.refs_1_ = f32[512,1536]{1,0:T(8,128)} collective-permute-done((f32[512,1536]{1,0:T(8,128)S(1)}, f32[512,1536]{1,0:T(8,128)}, u32[]{:S(2)}, u32[]{:S(2)}) %collective-permute-start.22) | collective-permute-done | bytes 3145760 | tf_op jit(solution)/shard_map/ppermute | solution.py:400
  794.3 67.4 %collective-permute-done.24.refs_2_ = f32[512,1536]{1,0:T(8,128)} collective-permute-done((f32[512,1536]{1,0:T(8,128)S(1)}, f32[512,1536]{1,0:T(8,128)}, u32[]{:S(2)}, u32[]{:S(2)}) %collective-permute-start.24) | collective-permute-done | bytes 3145760 | tf_op jit(solution)/shard_map/ppermute | solution.py:400
  861.7 10.6 %combine.3.base = f32[1536,1536]{1,0:T(8,128)} custom-call(f32[1]{0:T(128)S(6)} %div.10.factor, f32[1536,1536]{1,0:T(8,128)S(1)} %bitcast.1, f32[1536,1536]{1,0:T(8,128)} %collective-permute-done.20.refs_0_, f32[512,1536]{1,0:T(8,128)} %collective-permute-done.22.refs_1_, f32[512,1536]{1,0:T(8,128)} %collective-permute-done.24.refs_2_), custom_call_target="tpu_custom_call" | custom-call | flops 150994944 | bytes 37748736 | tf_op jit(solution)/shard_map/combine/pallas_call | solution.py:349
  872.3 52.0 %collective-permute-done.26.refs_0_ = f32[512,1536]{1,0:T(8,128)} collective-permute-done((f32[512,1536]{1,0:T(8,128)}, f32[512,1536]{1,0:T(8,128)}, u32[]{:S(2)}, u32[]{:S(2)}) %collective-permute-start.26) | collective-permute-done | bytes 3145760 | tf_op jit(solution)/shard_map/ppermute | solution.py:400
  924.3 4.9 add_rows.2
  (89 shorter events, 53.0 us)
Async XLA Ops:
  0.6 76.4 %collective-permute-start = (bf16[1536,1536]{1,0:T(8,128)(2,1)}, bf16[1536,1536]{1,0:T(8,128)(2,1)}, u32[]{:S(2)}, u32[]{:S(2)}) collective-permute-start(bf16[1536,1536]{1,0:T(8,128)(2,1)} %refs_2_.7), channel_id=1, source_target_pairs={{0,1},{1,0},{2,3},{3,2},{4,5},{5,4},{6,7},{7,6},{8,9},{9,8},{10,11... | collective-permute-start | bytes 14155784 | tf_op jit(solution)/shard_map/ppermute | solution.py:400
  7.9 69.1 %collective-permute-start.1 = (bf16[512,1536]{1,0:T(8,128)(2,1)S(1)}, bf16[512,1536]{1,0:T(8,128)(2,1)}, u32[]{:S(2)}, u32[]{:S(2)}) collective-permute-start(bf16[512,1536]{1,0:T(8,128)(2,1)S(1)} %get-tuple-element.119), channel_id=1, source_target_pairs={{0,2},{1,3},{2,0},{3,1},{4,6},{5,7},{6,4},{7,5},{8,10},{9,11},{10,... | collective-permute-start | bytes 4718600 | tf_op jit(solution)/shard_map/ppermute | solution.py:400
  7.9 128.2 %collective-permute-start.5 = (bf16[512,1536]{1,0:T(8,128)(2,1)}, bf16[512,1536]{1,0:T(8,128)(2,1)}, u32[]{:S(2)}, u32[]{:S(2)}) collective-permute-start(bf16[512,1536]{1,0:T(8,128)(2,1)} %get-tuple-element.117), channel_id=1, source_target_pairs={{0,2},{1,3},{2,0},{3,1},{4,6},{5,7},{6,4},{7,5},{8,10},{9,11},{10,... | collective-permute-start | bytes 4718600 | tf_op jit(solution)/shard_map/ppermute | solution.py:400
  10.2 128.0 %collective-permute-start.9 = (bf16[768,1536]{1,0:T(8,128)(2,1)S(1)}, bf16[768,1536]{1,0:T(8,128)(2,1)}, u32[]{:S(2)}, u32[]{:S(2)}) collective-permute-start(bf16[768,1536]{1,0:T(8,128)(2,1)S(1)} %get-tuple-element.115), channel_id=1, source_target_pairs={{0,8},{1,9},{2,10},{3,11},{4,12},{5,13},{6,14},{7,15},{8,0},{9,1},... | collective-permute-start | bytes 7077896 | tf_op jit(solution)/shard_map/ppermute | solution.py:400
  43.2 96.6 %collective-permute-start.7 = (bf16[768,1536]{1,0:T(8,128)(2,1)S(1)}, bf16[768,1536]{1,0:T(8,128)(2,1)}, u32[]{:S(2)}, u32[]{:S(2)}) collective-permute-start(bf16[768,1536]{1,0:T(8,128)(2,1)S(1)} %get-tuple-element.116), channel_id=1, source_target_pairs={{0,4},{1,5},{2,6},{3,7},{4,0},{5,1},{6,2},{7,3},{8,12},{9,13},{10,... | collective-permute-start | bytes 7077896 | tf_op jit(solution)/shard_map/ppermute | solution.py:400
  76.9 62.9 %collective-permute-start.4 = (bf16[512,1536]{1,0:T(8,128)(2,1)}, bf16[512,1536]{1,0:T(8,128)(2,1)}, u32[]{:S(2)}, u32[]{:S(2)}) collective-permute-start(bf16[512,1536]{1,0:T(8,128)(2,1)} %collective-permute-done.3.refs_4_.refs_6_.refs_2_), channel_id=1, source_target_pairs={{0,1},{1,0},{2,3},{3,2},{4,5},{5,4},{6,7},{7,6},{8,9},{9,8},{10,11... | collective-permute-start | bytes 4718600 | tf_op jit(solution)/shard_map/ppermute | solution.py:400
  77.0 63.3 %collective-permute-start.2 = (bf16[512,1536]{1,0:T(8,128)(2,1)}, bf16[512,1536]{1,0:T(8,128)(2,1)}, u32[]{:S(2)}, u32[]{:S(2)}) collective-permute-start(bf16[512,1536]{1,0:T(8,128)(2,1)} %collective-permute-done.1.refs_2_.refs_4_), channel_id=1, source_target_pairs={{0,1},{1,0},{2,3},{3,2},{4,5},{5,4},{6,7},{7,6},{8,9},{9,8},{10,11... | collective-permute-start | bytes 4718600 | tf_op jit(solution)/shard_map/ppermute | solution.py:400
  136.1 210.9 %collective-permute-start.12 = (bf16[768,1536]{1,0:T(8,128)(2,1)S(1)}, bf16[768,1536]{1,0:T(8,128)(2,1)}, u32[]{:S(2)}, u32[]{:S(2)}) collective-permute-start(bf16[768,1536]{1,0:T(8,128)(2,1)S(1)} %get-tuple-element.115), channel_id=1, source_target_pairs={{0,4},{1,5},{2,6},{3,7},{4,0},{5,1},{6,2},{7,3},{8,12},{9,13},{10,... | collective-permute-start | bytes 7077896 | tf_op jit(solution)/shard_map/ppermute | solution.py:400
  138.2 208.8 %collective-permute-start.11 = (bf16[768,1536]{1,0:T(8,128)(2,1)S(1)}, bf16[768,1536]{1,0:T(8,128)(2,1)}, u32[]{:S(2)}, u32[]{:S(2)}) collective-permute-start(bf16[768,1536]{1,0:T(8,128)(2,1)S(1)} %get-tuple-element.116), channel_id=1, source_target_pairs={{0,8},{1,9},{2,10},{3,11},{4,12},{5,13},{6,14},{7,15},{8,0},{9,1},... | collective-permute-start | bytes 7077896 | tf_op jit(solution)/shard_map/ppermute | solution.py:400
  139.8 100.5 %collective-permute-start.10 = (bf16[768,1536]{1,0:T(8,128)(2,1)}, bf16[768,1536]{1,0:T(8,128)(2,1)}, u32[]{:S(2)}, u32[]{:S(2)}) collective-permute-start(bf16[768,1536]{1,0:T(8,128)(2,1)} %collective-permute-done.9.refs_6_.refs_5_), channel_id=1, source_target_pairs={{0,4},{1,5},{2,6},{3,7},{4,0},{5,1},{6,2},{7,3},{8,12},{9,13},{10,... | collective-permute-start | bytes 7077896 | tf_op jit(solution)/shard_map/ppermute | solution.py:400
  140.3 101.4 %collective-permute-start.8 = (bf16[768,1536]{1,0:T(8,128)(2,1)}, bf16[768,1536]{1,0:T(8,128)(2,1)}, u32[]{:S(2)}, u32[]{:S(2)}) collective-permute-start(bf16[768,1536]{1,0:T(8,128)(2,1)} %collective-permute-done.7.refs_5_.refs_4_), channel_id=1, source_target_pairs={{0,8},{1,9},{2,10},{3,11},{4,12},{5,13},{6,14},{7,15},{8,0},{9,1},... | collective-permute-start | bytes 7077896 | tf_op jit(solution)/shard_map/ppermute | solution.py:400
  344.9 107.3 %collective-permute-start.13 = (f32[768,1536]{1,0:T(8,128)}, f32[768,1536]{1,0:T(8,128)}, u32[]{:S(2)}, u32[]{:S(2)}) collective-permute-start(f32[768,1536]{1,0:T(8,128)} %get-tuple-element.79), channel_id=1, source_target_pairs={{0,8},{1,9},{2,10},{3,11},{4,12},{5,13},{6,14},{7,15},{8,0},{9,1},... | collective-permute-start | bytes 14155784 | tf_op jit(solution)/shard_map/ppermute | solution.py:400
  346.5 105.7 %collective-permute-start.14 = (f32[768,1536]{1,0:T(8,128)}, f32[768,1536]{1,0:T(8,128)}, u32[]{:S(2)}, u32[]{:S(2)}) collective-permute-start(f32[768,1536]{1,0:T(8,128)} %get-tuple-element.80), channel_id=1, source_target_pairs={{0,4},{1,5},{2,6},{3,7},{4,0},{5,1},{6,2},{7,3},{8,12},{9,13},{10,... | collective-permute-start | bytes 14155784 | tf_op jit(solution)/shard_map/ppermute | solution.py:400
  450.2 156.8 %collective-permute-start.27 = (f32[768,1536]{1,0:T(8,128)}, f32[768,1536]{1,0:T(8,128)}, u32[]{:S(2)}, u32[]{:S(2)}) collective-permute-start(f32[768,1536]{1,0:T(8,128)} %get-tuple-element.109), channel_id=1, source_target_pairs={{0,8},{1,9},{2,10},{3,11},{4,12},{5,13},{6,14},{7,15},{8,0},{9,1},... | collective-permute-start | bytes 14155784 | tf_op jit(solution)/shard_map/ppermute | solution.py:400
  450.5 160.1 %collective-permute-start.28 = (f32[768,1536]{1,0:T(8,128)}, f32[768,1536]{1,0:T(8,128)}, u32[]{:S(2)}, u32[]{:S(2)}) collective-permute-start(f32[768,1536]{1,0:T(8,128)} %get-tuple-element.110), channel_id=1, source_target_pairs={{0,4},{1,5},{2,6},{3,7},{4,0},{5,1},{6,2},{7,3},{8,12},{9,13},{10,... | collective-permute-start | bytes 14155784 | tf_op jit(solution)/shard_map/ppermute | solution.py:400
  577.9 283.8 %collective-permute-start.20 = (f32[1536,1536]{1,0:T(8,128)}, f32[1536,1536]{1,0:T(8,128)}, u32[]{:S(2)}, u32[]{:S(2)}) collective-permute-start(f32[1536,1536]{1,0:T(8,128)} %get-tuple-element.101), channel_id=1, source_target_pairs={{0,1},{1,0},{2,3},{3,2},{4,5},{5,4},{6,7},{7,6},{8,9},{9,8},{10,11... | collective-permute-start | bytes 28311560 | tf_op jit(solution)/shard_map/ppermute | solution.py:400
  578.0 44.6 %collective-permute-start.21 = (f32[512,1536]{1,0:T(8,128)}, f32[512,1536]{1,0:T(8,128)S(1)}, u32[]{:S(2)}, u32[]{:S(2)}) collective-permute-start(f32[512,1536]{1,0:T(8,128)} %get-tuple-element.103), channel_id=1, source_target_pairs={{0,1},{1,0},{2,3},{3,2},{4,5},{5,4},{6,7},{7,6},{8,9},{9,8},{10,11... | collective-permute-start | bytes 9437192 | tf_op jit(solution)/shard_map/ppermute | solution.py:400
  610.6 114.1 %collective-permute-start.25 = (f32[512,1536]{1,0:T(8,128)}, f32[512,1536]{1,0:T(8,128)S(1)}, u32[]{:S(2)}, u32[]{:S(2)}) collective-permute-start(f32[512,1536]{1,0:T(8,128)} %get-tuple-element.107), channel_id=1, source_target_pairs={{0,1},{1,0},{2,3},{3,2},{4,5},{5,4},{6,7},{7,6},{8,9},{9,8},{10,11... | collective-permute-start | bytes 9437192 | tf_op jit(solution)/shard_map/ppermute | solution.py:400
  622.3 105.3 %collective-permute-start.29 = (f32[512,1536]{1,0:T(8,128)}, f32[512,1536]{1,0:T(8,128)S(1)}, u32[]{:S(2)}, u32[]{:S(2)}) collective-permute-start(f32[512,1536]{1,0:T(8,128)} %get-tuple-element.111), channel_id=1, source_target_pairs={{0,4},{1,5},{2,6},{3,7},{4,0},{5,1},{6,2},{7,3},{8,12},{9,13},{10,... | collective-permute-start | bytes 9437192 | tf_op jit(solution)/shard_map/ppermute | solution.py:400
  622.6 108.1 %collective-permute-start.30 = (f32[512,1536]{1,0:T(8,128)}, f32[512,1536]{1,0:T(8,128)S(1)}, u32[]{:S(2)}, u32[]{:S(2)}) collective-permute-start(f32[512,1536]{1,0:T(8,128)} %get-tuple-element.112), channel_id=1, source_target_pairs={{0,8},{1,9},{2,10},{3,11},{4,12},{5,13},{6,14},{7,15},{8,0},{9,1},... | collective-permute-start | bytes 9437192 | tf_op jit(solution)/shard_map/ppermute | solution.py:400
  624.3 98.9 %collective-permute-start.31 = (f32[256,1536]{1,0:T(8,128)}, f32[256,1536]{1,0:T(8,128)S(1)}, u32[]{:S(2)}, u32[]{:S(2)}) collective-permute-start(f32[256,1536]{1,0:T(8,128)} %get-tuple-element.113), channel_id=1, source_target_pairs={{0,4},{1,5},{2,6},{3,7},{4,0},{5,1},{6,2},{7,3},{8,12},{9,13},{10,... | collective-permute-start | bytes 4718600 | tf_op jit(solution)/shard_map/ppermute | solution.py:400
  723.2 71.1 %collective-permute-start.22 = (f32[512,1536]{1,0:T(8,128)S(1)}, f32[512,1536]{1,0:T(8,128)}, u32[]{:S(2)}, u32[]{:S(2)}) collective-permute-start(f32[512,1536]{1,0:T(8,128)S(1)} %add.33), channel_id=1, source_target_pairs={{0,2},{1,3},{2,0},{3,1},{4,6},{5,7},{6,4},{7,5},{8,10},{9,11},{10,... | collective-permute-start | bytes 9437192 | tf_op jit(solution)/shard_map/ppermute | solution.py:400
  724.7 137.0 %collective-permute-start.24 = (f32[512,1536]{1,0:T(8,128)S(1)}, f32[512,1536]{1,0:T(8,128)}, u32[]{:S(2)}, u32[]{:S(2)}) collective-permute-start(f32[512,1536]{1,0:T(8,128)S(1)} %add.34), channel_id=1, source_target_pairs={{0,2},{1,3},{2,0},{3,1},{4,6},{5,7},{6,4},{7,5},{8,10},{9,11},{10,... | collective-permute-start | bytes 9437192 | tf_op jit(solution)/shard_map/ppermute | solution.py:400
  729.2 195.1 %collective-permute-start.26 = (f32[512,1536]{1,0:T(8,128)}, f32[512,1536]{1,0:T(8,128)}, u32[]{:S(2)}, u32[]{:S(2)}) collective-permute-start(f32[512,1536]{1,0:T(8,128)} %add.35), channel_id=1, source_target_pairs={{0,2},{1,3},{2,0},{3,1},{4,6},{5,7},{6,4},{7,5},{8,10},{9,11},{10,... | collective-permute-start | bytes 9437192 | tf_op jit(solution)/shard_map/ppermute | solution.py:400
  (19 other events, 622.5 us)
